TPU v7x, 512 devices: a 4x2x32 block of a 4x8x32 slice. The times are simulated.
512 devices in a mesh: groups: 2 (over y), gx: 64 (over z, core), gy: 4 (over x).
Axes of the slice: x: 4, y: 2, z: 32, core: 2. Of those that a mesh axis runs over, the one named last changes fastest.
The devices are a block of a 4x8x32 slice.
Arguments:
- thermal_deviation: float32 [32, 256, 8192], P('groups', 'gy', 'gx'), parts along dimension 0, may hold values from -6 to 6
- brine_content: float32 [32, 256, 8192], P('groups', 'gy', 'gx'), parts along dimension 0, may hold values from 0.2 to 2.4
- current_components: float32 [4, 16, 256, 8192], P('groups', None, 'gy', 'gx'), parts along dimension 0, may hold values from -4 to 4
- sea_indicator: int32 [256, 8192], P('gy', 'gx'), may hold values from 0 to 1, as said below
- flooded_layer_number: int32 [256, 8192], P('gy', 'gx'), may hold values from 1 to 16
- footprint_square_metres: float32 [256, 8192], P('gy', 'gx'), may hold values from 0.5 to 5
- rainfall_input: float32 [256, 8192], P('gy', 'gx'), may hold values from -2 to 3.5
- seam_partner_index: int32 [8192], P('gx'), may hold values from 0 to 8191, as said below
Outputs:
- temperature_next: float32 [32, 256, 8192], P('groups', 'gy', 'gx'), parts along dimension 0
- salinity_next: float32 [32, 256, 8192], P('groups', 'gy', 'gx'), parts along dimension 0
There are 2 independent parts, one for each index of `groups`. A program takes and returns all parts, laid end to end along the dimension named above; an argument that names none is the same for every part. Nothing has to cross between parts.
Inputs may be any that keep to these rules, and one draw needn't show every extreme that they name: `sea_indicator`: at least one column is ocean. seam_partner_index[x] = (s - x) mod 8192 for one s of each draw with s mod 128 = 127; the map is its own inverse and has no fixed point.
All inputs are finite; a program needn't handle non-finite values.
Results may differ from a plain program's by a relative error of at most 0.00002.
Values sent between devices are 32-bit elements; how exact they have to be, the bound alone decides.
No kernel may reach another device: no remote copies, remote signals or barrier semaphores. Data moves between devices by JAX's collectives and lax.ppermute only.
A program may use at most 64 MiB of HBM per device.

v0:
```python
import jax
import jax.numpy as jnp
from jax import lax
from jax.experimental import pallas as pl
from jax.experimental.pallas import tpu as pltpu
from jax.sharding import Mesh
from jax.sharding import PartitionSpec as P

time_step = 0.25
diffusivity = 0.5
vertical_mixing = 0.3
top_thickness = 0.5

VMEM = pl.BlockSpec(memory_space=pltpu.VMEM)
LANES = 128
CORES = 2
GX = ("chip", "core")
NEAR = ("core", "gy")


def lane_of(shape):
    return lax.broadcasted_iota(jnp.int32, shape, len(shape) - 1)


def sums_kernel(surface, sea, area, rain, out):
    wet_area = area[...] * sea[...].astype(jnp.float32)
    salt = wet_area * surface[0]
    rain_now = rain[...]
    lane = lane_of((1, LANES))
    packed = jnp.zeros((1, LANES), jnp.float32)
    for place, field in enumerate((wet_area, wet_area * rain_now, salt * rain_now, salt)):
        total = jnp.sum(jnp.sum(field, axis=0, keepdims=True), axis=1, keepdims=True)
        packed = jnp.where(lane == place, total, packed)
    out[...] = jnp.broadcast_to(packed[None], out.shape)


def local_sums(brine, sea, area, rain, copies):
    rows, width = sea.shape
    plane = pl.BlockSpec((rows, width), lambda i: (0, 0))
    return pl.pallas_call(
        sums_kernel,
        grid=(1,),
        in_specs=[pl.BlockSpec((1, rows, width), lambda i: (0, 0, 0)), plane, plane, plane],
        out_specs=pl.BlockSpec((copies, 1, LANES), lambda i: (0, 0, 0)),
        out_shape=jax.ShapeDtypeStruct((copies, 1, LANES), jnp.float32),
        name="local_sums",
    )(brine, sea, area, rain)


def mirrored(rows):
    lane = lane_of(rows.shape)
    bit = 1
    while bit < LANES:
        low = (lane // bit) % 2 == 0
        rows = jnp.where(low, pltpu.roll(rows, LANES - bit, 1), pltpu.roll(rows, bit, 1))
        bit *= 2
    return rows


def column_pack(planes, lane_number):
    lane = lane_of((8, LANES))
    blocks = planes[0].shape[0] // 8
    packed = jnp.zeros((8, LANES), jnp.float32)
    for level, plane in enumerate(planes):
        for block in range(blocks):
            place = level * blocks + block
            tile = plane[8 * block : 8 * block + 8]
            moved = pltpu.roll(tile, (place - lane_number) % LANES, 1)
            packed = jnp.where(lane == place, moved, packed)
    return packed


def pack_kernel(heat, salt, currents, sea, layers, west, east, south, north, fold):
    levels, rows, _ = heat.shape
    depth = (sea[...] * layers[...]).astype(jnp.float32)
    heat_planes = [heat[k] for k in range(levels)]
    salt_planes = [salt[k] for k in range(levels)]
    speed_planes = [currents[0, k] for k in range(levels)]
    depth_planes = [depth] * levels
    west[0:8] = column_pack(heat_planes, 0)
    west[8:16] = column_pack(salt_planes, 0)
    west[16:24] = column_pack(depth_planes, 0)
    east[0:8] = column_pack(heat_planes, LANES - 1)
    east[8:16] = column_pack(salt_planes, LANES - 1)
    east[16:24] = column_pack(depth_planes, LANES - 1)
    east[24:32] = column_pack(speed_planes, LANES - 1)
    last = rows - 1
    for k in range(levels):
        south[k : k + 1] = heat[k, 0:1]
        south[levels + k : levels + k + 1] = salt[k, 0:1]
        north[k : k + 1] = heat[k, last:rows]
        north[levels + k : levels + k + 1] = salt[k, last:rows]
        north[2 * levels + 8 + k : 2 * levels + 9 + k] = currents[1, k, last:rows]
    south[2 * levels : 2 * levels + 8] = jnp.broadcast_to(depth[0:1], (8, LANES))
    north[2 * levels : 2 * levels + 8] = jnp.broadcast_to(depth[last:rows], (8, LANES))
    turned = mirrored(north[...])
    fold[...] = turned
    west[24:] = turned
    east[32:] = turned


def packs(heat, salt, currents, sea, layers):
    levels, _, _ = heat.shape
    north = 3 * levels + 8
    shapes = (24 + north, 32 + north, 2 * levels + 8, north, north)
    return pl.pallas_call(
        pack_kernel,
        in_specs=[VMEM] * 5,
        out_specs=[VMEM] * 5,
        out_shape=[jax.ShapeDtypeStruct((n, LANES), jnp.float32) for n in shapes],
        name="edge_packs",
    )(heat, salt, currents, sea, layers)


def open_flux(near, far, forward, backward):
    return forward * near + backward * far - diffusivity * (far - near)


def edge_flux(near, far, speed, near_depth, far_depth, level):
    wet = (level < jnp.minimum(near_depth, far_depth)).astype(jnp.float32)
    return wet * open_flux(near, far, jnp.maximum(speed, 0.0), jnp.minimum(speed, 0.0))


def step_kernel(
    heat, salt, currents, sea, layers, area,
    west_own, east_own, west_halo, east_halo, south_halo, north_halo,
    heat_out, salt_out,
):
    levels, rows, _ = heat.shape
    blocks = rows // 8
    lane = lane_of((rows, LANES))
    row = lax.broadcasted_iota(jnp.int32, (rows, LANES), 0)
    first_lane, last_lane = lane == 0, lane == LANES - 1
    first_row, last_row = row == 0, row == rows - 1
    depth = (sea[...] * layers[...]).astype(jnp.float32)
    base = 2 * levels
    south_depth = south_halo[base : base + 1]
    depth_north = jnp.where(last_row, north_halo[base : base + 1], pltpu.roll(depth, rows - 1, 0))
    open_north = jnp.minimum(depth, depth_north)
    open_south = jnp.minimum(depth[0:1], south_depth)
    open_east = jnp.where(last_lane, 0.0, jnp.minimum(depth, pltpu.roll(depth, LANES - 1, 1)))
    per_area = time_step / area[...]
    edge_level = (lane_of((8, LANES)) // blocks).astype(jnp.float32)
    west_edge, east_edge = [], []
    for f in range(2):
        own_west, own_east = west_own[8 * f : 8 * f + 8], east_own[8 * f : 8 * f + 8]
        west_edge.append(
            edge_flux(west_halo[8 * f : 8 * f + 8], own_west, west_halo[24:32], west_halo[16:24], west_own[16:24], edge_level)
        )
        east_edge.append(
            edge_flux(own_east, east_halo[8 * f : 8 * f + 8], east_own[24:32], east_own[16:24], east_halo[16:24], edge_level)
        )
    fields = (heat, salt)

    def one_level(k, above):
        level = k.astype(jnp.float32)
        east_speed, north_speed = currents[0, k], currents[1, k]
        south_speed = south_halo[pl.ds(base + 8 + k, 1)]
        east_up, east_down = jnp.maximum(east_speed, 0.0), jnp.minimum(east_speed, 0.0)
        north_up, north_down = jnp.maximum(north_speed, 0.0), jnp.minimum(north_speed, 0.0)
        east_wet = level < open_east
        north_wet = level < open_north
        wet = level < depth
        below_wet = level + 1.0 < depth
        passed = []
        for f in range(2):
            cells = fields[f][k]
            at = f * levels + k
            east_flux = jnp.where(
                east_wet, open_flux(cells, pltpu.roll(cells, LANES - 1, 1), east_up, east_down), 0.0
            )
            west_flux = pltpu.roll(east_flux, 1, 1)
            west_columns, east_columns = [], []
            for block in range(blocks):
                place = k * blocks + block
                west_columns.append(pltpu.roll(west_edge[f], (LANES - place) % LANES, 1))
                east_columns.append(pltpu.roll(east_edge[f], LANES - 1 - place, 1))
            west_flux = jnp.where(first_lane, jnp.concatenate(west_columns, axis=0), west_flux)
            east_flux = jnp.where(last_lane, jnp.concatenate(east_columns, axis=0), east_flux)
            northern = jnp.where(last_row, north_halo[pl.ds(at, 1)], pltpu.roll(cells, rows - 1, 0))
            north_flux = jnp.where(north_wet, open_flux(cells, northern, north_up, north_down), 0.0)
            first_flux = edge_flux(
                south_halo[pl.ds(at, 1)], cells[0:1], south_speed, open_south, open_south, level
            )
            south_flux = jnp.where(first_row, first_flux, pltpu.roll(north_flux, 1, 0))
            next_cells = fields[f][jnp.minimum(k + 1, levels - 1)]
            below = jnp.where(below_wet, vertical_mixing * (cells - next_cells), 0.0)
            change = per_area * (west_flux - east_flux + south_flux - north_flux) + time_step * (above[f] - below)
            (heat_out, salt_out)[f][k] = cells + jnp.where(wet, change, 0.0)
            passed.append(below)
        return tuple(passed)

    nothing = jnp.zeros((rows, LANES), jnp.float32)
    lax.fori_loop(0, levels, one_level, (nothing, nothing))


def tracer_step(*arrays):
    heat = arrays[0]
    return pl.pallas_call(
        step_kernel,
        in_specs=[VMEM] * 12,
        out_specs=[VMEM] * 2,
        out_shape=[jax.ShapeDtypeStruct(heat.shape, jnp.float32)] * 2,
        name="tracer_step",
    )(*arrays)


def fold_kernel(heat_next, salt_next, own, fold, area, heat_out, salt_out):
    levels, band, _ = heat_next.shape
    base = 2 * levels
    level = lax.broadcasted_iota(jnp.int32, (levels, LANES), 0).astype(jnp.float32)
    per_area = time_step / area[band - 1 : band]
    speed = 0.5 * (own[base + 8 :] - fold[base + 8 :])
    last = lax.broadcasted_iota(jnp.int32, (band, LANES), 0) == band - 1
    for f, (before, after) in enumerate(((heat_next, heat_out), (salt_next, salt_out))):
        flux = edge_flux(
            own[f * levels : f * levels + levels], fold[f * levels : f * levels + levels], speed,
            own[base : base + 1], fold[base : base + 1], level,
        )
        leaving = per_area * flux
        for k in range(levels):
            after[k] = before[k] - jnp.where(last, leaving[k : k + 1], 0.0)


def close_fold(heat_next, salt_next, own, fold, area):
    levels, rows, width = heat_next.shape
    band = pl.BlockSpec((levels, 8, width), lambda i: (0, rows // 8 - 1, 0))
    whole = pl.BlockSpec(own.shape, lambda i: (0, 0))
    return pl.pallas_call(
        fold_kernel,
        grid=(1,),
        in_specs=[band, band, whole, whole, pl.BlockSpec((8, width), lambda i: (rows // 8 - 1, 0))],
        out_specs=[band, band],
        out_shape=[jax.ShapeDtypeStruct(heat_next.shape, jnp.float32)] * 2,
        input_output_aliases={0: 0, 1: 1},
        name="close_fold",
    )(heat_next, salt_next, own, fold, area)


def final_kernel(salt_next, surface, rain, sea, totals, out):
    lane = lane_of((1, LANES))

    def total(place):
        return jnp.sum(jnp.where(lane == place, totals[...], 0.0), axis=1, keepdims=True)

    total_area, total_fresh, salt_fresh, salt_only = (total(place) for place in range(4))
    mean_fresh = total_fresh / total_area
    total_salt = salt_fresh - mean_fresh * salt_only
    balanced = rain[...] - mean_fresh
    virtual = -surface[0] * balanced + total_salt / total_area
    wet = (sea[...] > 0).astype(jnp.float32)
    out[0] = salt_next[0] + time_step / top_thickness * virtual * wet


def add_virtual(salt_next, brine, rain, sea, totals):
    _, rows, width = salt_next.shape
    plane = pl.BlockSpec((rows, width), lambda i: (0, 0))
    top = pl.BlockSpec((1, rows, width), lambda i: (0, 0, 0))
    return pl.pallas_call(
        final_kernel,
        grid=(1,),
        in_specs=[top, top, plane, plane, pl.BlockSpec((1, LANES), lambda i: (0, 0))],
        out_specs=top,
        out_shape=jax.ShapeDtypeStruct(salt_next.shape, jnp.float32),
        input_output_aliases={0: 0},
        name="add_virtual",
    )(salt_next, brine, rain, sea, totals)


def all_sum(copies, axes):
    return jnp.sum(lax.all_to_all(copies, axes, 0, 0, tiled=True), axis=0)


def along(block, axis, by, closed):
    count = lax.axis_size(axis)
    pairs = [(i, (i + by) % count) for i in range(count) if closed or i + by in range(count)]
    return lax.ppermute(block, axis, pairs)


def fold_exchange(own, from_west, from_east, seam, width, beside):
    around, height = lax.axis_size(GX), lax.axis_size("gy")
    centre = (seam[0] // width + lax.axis_index(GX)) % around
    part = (centre + 1) % 3
    held = jnp.where(part == 0, from_west, jnp.where(part == 2, from_east, own))

    def mirror(coarse):
        pairs = [
            (i * height + height - 1, (3 * coarse - i) % around * height + height - 1) for i in range(around)
        ]

        def branch(rows, arrays):
            return lax.ppermute(rows, GX + ("gy",), pairs), beside(*arrays)

        return branch

    return (centre + 1) // 3, [mirror(coarse) for coarse in range((around + 2) // 3)], held


def shards(heat, brine, currents, sea, layers, area, rain, seam):
    _, _, width = heat.shape
    sums = local_sums(brine, sea, area, rain, lax.axis_size(NEAR))
    plane = all_sum(sums, NEAR)
    west_own, east_own, south_own, north_own, fold_own = packs(heat, brine, currents, sea, layers)
    plane, west_own, east_own, south_own, north_own = lax.optimization_barrier(
        (plane, west_own, east_own, south_own, north_own)
    )
    totals = all_sum(jnp.broadcast_to(plane[None], (lax.axis_size("chip"),) + plane.shape), "chip")
    west_halo = along(east_own, GX, 1, True)
    east_halo = along(west_own, GX, -1, True)
    south_halo = along(north_own, "gy", 1, False)
    north_halo = along(south_own, "gy", -1, False)
    place, branches, held = fold_exchange(fold_own, west_halo[32:], east_halo[24:], seam, width, tracer_step)
    arrays = (
        heat, brine, currents, sea, layers, area,
        west_own, east_own, west_halo, east_halo, south_halo, north_halo,
    )
    fold_halo, (heat_next, salt_next) = lax.switch(place, branches, held, arrays)
    heat_next, salt_next = close_fold(heat_next, salt_next, north_own, fold_halo, area)
    return heat_next, add_virtual(salt_next, brine, rain, sea, totals)


def solution(mesh):
    chips = mesh.shape["gx"] // CORES
    split = Mesh(
        mesh.devices.reshape(mesh.shape["groups"], chips, CORES, mesh.shape["gy"]), ("groups",) + GX + ("gy",)
    )
    cells = P("groups", "gy", GX)
    plane = P("gy", GX)
    in_specs = (cells, cells, P("groups", None, "gy", GX), plane, plane, plane, plane, P(GX))
    return jax.shard_map(
        shards, mesh=split, in_specs=in_specs, out_specs=(cells, cells), check_vma=False
    )
```

profile of v0, /device:TPU:38, one launch (start us, length us, event | category | flops | bytes accessed | tf_op | source)
XLA Modules:
  0.0 95.3 jit_solution(17649941730675683546)
XLA Ops:
  0.6 0.0 copy-start.3
  0.6 0.0 copy-start.1
  0.7 0.0 copy-start.5
  0.7 1.6 %local_sums.1 = f32[8,1,128]{2,1,0:T(1,128)} custom-call(f32[16,64,128]{2,1,0:T(8,128)} %surface.3, s32[64,128]{1,0:T(8,128)} %sea.5, f32[64,128]{1,0:T(8,128)} %area.3, f32[64,128]{1,0:T(8,128)} %rain.3), custom_call_target="tpu_custom_call" | custom-call | tf_op jit(solution)/shard_map/local_sums/pallas_call | solution.py:40
  2.2 43.3 %all-to-all-start = ((f32[8,1,128]{2,1,0:T(1,128)}), f32[8,1,128]{2,1,0:T(1,128)S(1)}, u32[]{:S(2)}, u32[]{:S(2)}) async-start(f32[8,1,128]{2,1,0:T(1,128)} %local_sums.1), calls=%async_computation | async-start | bytes 8192 | tf_op jit(solution)/shard_map/all_to_all | solution.py:271
  45.5 0.0 copy-done.3
  45.5 0.0 copy-done.1
  45.5 0.0 copy-done.5
  45.5 0.0 copy-start
  45.5 0.0 copy-start.2
  45.5 3.4 %edge_packs.1 = (f32[80,128]{1,0:T(8,128)S(1)}, f32[88,128]{1,0:T(8,128)S(1)}, f32[40,128]{1,0:T(8,128)}, f32[56,128]{1,0:T(8,128)}, f32[56,128]{1,0:T(8,128)}) custom-call(f32[16,64,128]{2,1,0:T(8,128)} %heat.1, f32[16,64,128]{2,1,0:T(8,128)S(1)} %copy-done.1, f32[2,16,64,128]{3,2,1,0:T(8,128)} %currents.1, s32[64,128]{1,0:T(8,128)S(1)} %copy-done.3, ...), custom_call_target="tpu_custom_call" | custom-call | tf_op jit(solution)/shard_map/edge_packs/pallas_call | solution.py:106
  48.9 0.0 all-to-all-done
  49.0 0.2 collective-permute-start.22
  49.2 4.4 %collective-permute-start.23 = (f32[80,128]{1,0:T(8,128)S(1)}, f32[80,128]{1,0:T(8,128)S(1)}, u32[]{:S(2)}, u32[]{:S(2)}) collective-permute-start(f32[80,128]{1,0:T(8,128)S(1)} %get-tuple-element.924), channel_id=1, source_target_pairs={{0,252},{4,0},{8,4},{12,8},{16,12},{20,16},{24,20},{28,24},{32,28}... | collective-permute-start | bytes 122888 | tf_op jit(solution)/shard_map/ppermute | solution.py:277
  53.6 0.0 copy-start.10
  53.6 0.7 copy-done.10
  54.4 0.0 copy-start.11
  54.5 0.0 copy-start.9
  54.5 0.0 copy-start.8
  54.5 0.6 broadcast_in_dim.9
  55.1 4.7 %all-to-all-start.1 = ((f32[32,1,128]{2,1,0:T(1,128)}), f32[32,1,128]{2,1,0:T(1,128)S(1)}, u32[]{:S(2)}, u32[]{:S(2)}) async-start(f32[32,1,128]{2,1,0:T(1,128)} %broadcast_in_dim.9), calls=%async_computation.1 | async-start | bytes 32768 | tf_op jit(solution)/shard_map/all_to_all | solution.py:271
  59.8 0.0 copy-done.11
  59.8 2.8 %collective-permute-start.25 = (f32[40,128]{1,0:T(8,128)S(1)}, f32[40,128]{1,0:T(8,128)S(1)}, u32[]{:S(2)}, u32[]{:S(2)}) collective-permute-start(f32[40,128]{1,0:T(8,128)S(1)} %copy-done.11), channel_id=1, source_target_pairs={{1,0},{2,1},{3,2},{5,4},{6,5},{7,6},{9,8},{10,9},{11,10},{13,12},{... | collective-permute-start | bytes 61448 | tf_op jit(solution)/shard_map/ppermute | solution.py:277
  62.6 0.0 copy-done.9
  62.6 1.3 %collective-permute-start.24 = (f32[56,128]{1,0:T(8,128)S(1)}, f32[56,128]{1,0:T(8,128)S(1)}, u32[]{:S(2)}, u32[]{:S(2)}) collective-permute-start(f32[56,128]{1,0:T(8,128)S(1)} %copy-done.9), channel_id=1, source_target_pairs={{0,1},{1,2},{2,3},{4,5},{5,6},{6,7},{8,9},{9,10},{10,11},{12,13},{... | collective-permute-start | bytes 86024 | tf_op jit(solution)/shard_map/ppermute | solution.py:277
  63.9 0.0 collective-permute-done.23
  63.9 0.0 collective-permute-done.22
  63.9 0.0 copy-done.8
  63.9 0.0 copy-start.4
  64.0 0.1 collective-permute-done.25
  64.1 4.3 %collective-permute-done.24 = f32[56,128]{1,0:T(8,128)S(1)} collective-permute-done((f32[56,128]{1,0:T(8,128)S(1)}, f32[56,128]{1,0:T(8,128)S(1)}, u32[]{:S(2)}, u32[]{:S(2)}) %collective-permute-start.24) | collective-permute-done | bytes 28704 | tf_op jit(solution)/shard_map/ppermute | solution.py:277
  68.4 0.0 copy-done
  68.4 0.0 copy-done.2
  68.4 0.0 copy-done.4
  68.4 23.8 %conditional.1 = (f32[56,128]{1,0:T(8,128)}, f32[16,64,128]{2,1,0:T(8,128)S(1)}, f32[16,64,128]{2,1,0:T(8,128)S(1)}) conditional(s32[]{:T(128)} %clamp.3, (f32[56,128]{1,0:T(8,128)S(1)}, f32[16,64,128]{2,1,0:T(8,128)S(1)}, f32[16,64,128]{2,1,0:T(8,128)S(1)}, f32[2,16,64,128]{3,2,1,0:T(8,128)S(1)}, ...), branch_computations={%region_1.0_spmd, %region_2.3_spmd, %region_3.4_spmd, %region_4.5_... | conditional | bytes 114752 | solution.py:317
  68.4 18.7 %collective-permute-start.11 = (f32[56,128]{1,0:T(8,128)S(1)}, f32[56,128]{1,0:T(8,128)}, u32[]{:S(2)}, u32[]{:S(2)}) collective-permute-start(f32[56,128]{1,0:T(8,128)S(1)} %get-tuple-element.737), channel_id=1, source_target_pairs={{3,135},{7,131},{11,127},{15,123},{19,119},{23,115},{27,111},{31,1... | collective-permute-start | bytes 86024 | tf_op jit(solution)/shard_map/cond/branch_11_fun/ppermute | solution.py:292
  87.2 2.8 %tracer_step.33 = (f32[16,64,128]{2,1,0:T(8,128)S(1)}, f32[16,64,128]{2,1,0:T(8,128)S(1)}) custom-call(f32[16,64,128]{2,1,0:T(8,128)S(1)} %get-tuple-element.738.heat, f32[16,64,128]{2,1,0:T(8,128)S(1)} %get-tuple-element.739.salt, f32[2,16,64,128]{3,2,1,0:T(8,128)S(1)} %get-tuple-element.740.currents, s32[64,128]{1,0:T(8,128)S(1)} %get-tuple-element.741.sea, ...), custom_call_target="tpu_custom_call" | custom-call | tf_op jit(solution)/shard_map/cond/branch_11_fun/tracer_step/pallas_call | solution.py:199
  90.0 2.2 %collective-permute-done.11 = f32[56,128]{1,0:T(8,128)} collective-permute-done((f32[56,128]{1,0:T(8,128)S(1)}, f32[56,128]{1,0:T(8,128)}, u32[]{:S(2)}, u32[]{:S(2)}) %collective-permute-start.11) | collective-permute-done | bytes 28704 | tf_op jit(solution)/shard_map/cond/branch_11_fun/ppermute | solution.py:292
  92.3 0.8 close_fold.1
  93.1 0.0 copy-start.7
  93.1 0.0 all-to-all-done.1
  93.1 0.6 reduce_sum.24
  93.7 0.9 add_virtual.1
  94.5 0.0 copy-done.7
  94.6 0.0 copy-start.6
  94.6 0.8 copy-done.6
  (2 shorter events, 0.0 us)
Async XLA Ops:
  0.6 44.8 %copy-start.3 = (s32[64,128]{1,0:T(8,128)S(1)}, s32[64,128]{1,0:T(8,128)}, u32[]{:S(2)}) copy-start(s32[64,128]{1,0:T(8,128)} %sea.5) | copy-start | bytes 98308
  0.6 44.8 %copy-start.1 = (f32[16,64,128]{2,1,0:T(8,128)S(1)}, f32[16,64,128]{2,1,0:T(8,128)}, u32[]{:S(2)}) copy-start(f32[16,64,128]{2,1,0:T(8,128)} %surface.3) | copy-start | bytes 1572868
  0.7 44.8 %copy-start.5 = (s32[64,128]{1,0:T(8,128)S(1)}, s32[64,128]{1,0:T(8,128)}, u32[]{:S(2)}) copy-start(s32[64,128]{1,0:T(8,128)} %layers.1) | copy-start | bytes 98308
  2.2 46.7 %all-to-all-start = ((f32[8,1,128]{2,1,0:T(1,128)}), f32[8,1,128]{2,1,0:T(1,128)S(1)}, u32[]{:S(2)}, u32[]{:S(2)}) async-start(f32[8,1,128]{2,1,0:T(1,128)} %local_sums.1), calls=%async_computation | async-start | bytes 8192 | tf_op jit(solution)/shard_map/all_to_all | solution.py:271
  45.5 22.9 %copy-start = (f32[2,16,64,128]{3,2,1,0:T(8,128)S(1)}, f32[2,16,64,128]{3,2,1,0:T(8,128)}, u32[]{:S(2)}) copy-start(f32[2,16,64,128]{3,2,1,0:T(8,128)} %currents.1) | copy-start | bytes 3145732
  45.5 22.9 %copy-start.2 = (f32[16,64,128]{2,1,0:T(8,128)S(1)}, f32[16,64,128]{2,1,0:T(8,128)}, u32[]{:S(2)}) copy-start(f32[16,64,128]{2,1,0:T(8,128)} %heat.1) | copy-start | bytes 1572868
  49.0 15.0 %collective-permute-start.22 = (f32[88,128]{1,0:T(8,128)S(1)}, f32[88,128]{1,0:T(8,128)S(1)}, u32[]{:S(2)}, u32[]{:S(2)}) collective-permute-start(f32[88,128]{1,0:T(8,128)S(1)} %get-tuple-element.923), channel_id=1, source_target_pairs={{0,4},{4,8},{8,12},{12,16},{16,20},{20,24},{24,28},{28,32},{32,36}... | collective-permute-start | bytes 135176 | tf_op jit(solution)/shard_map/ppermute | solution.py:277
  49.2 14.7 %collective-permute-start.23 = (f32[80,128]{1,0:T(8,128)S(1)}, f32[80,128]{1,0:T(8,128)S(1)}, u32[]{:S(2)}, u32[]{:S(2)}) collective-permute-start(f32[80,128]{1,0:T(8,128)S(1)} %get-tuple-element.924), channel_id=1, source_target_pairs={{0,252},{4,0},{8,4},{12,8},{16,12},{20,16},{24,20},{28,24},{32,28}... | collective-permute-start | bytes 122888 | tf_op jit(solution)/shard_map/ppermute | solution.py:277
  53.6 0.7 copy-start.10
  54.4 5.3 %copy-start.11 = (f32[40,128]{1,0:T(8,128)S(1)}, f32[40,128]{1,0:T(8,128)}, u32[]{:S(2)}) copy-start(f32[40,128]{1,0:T(8,128)} %get-tuple-element.927) | copy-start | bytes 61444
  54.5 8.1 %copy-start.9 = (f32[56,128]{1,0:T(8,128)S(1)}, f32[56,128]{1,0:T(8,128)}, u32[]{:S(2)}) copy-start(f32[56,128]{1,0:T(8,128)} %get-tuple-element.926.own) | copy-start | bytes 86020
  54.5 9.5 %copy-start.8 = (f32[56,128]{1,0:T(8,128)S(1)}, f32[56,128]{1,0:T(8,128)}, u32[]{:S(2)}) copy-start(f32[56,128]{1,0:T(8,128)} %get-tuple-element.925) | copy-start | bytes 86020
  55.1 38.0 %all-to-all-start.1 = ((f32[32,1,128]{2,1,0:T(1,128)}), f32[32,1,128]{2,1,0:T(1,128)S(1)}, u32[]{:S(2)}, u32[]{:S(2)}) async-start(f32[32,1,128]{2,1,0:T(1,128)} %broadcast_in_dim.9), calls=%async_computation.1 | async-start | bytes 32768 | tf_op jit(solution)/shard_map/all_to_all | solution.py:271
  59.8 4.3 %collective-permute-start.25 = (f32[40,128]{1,0:T(8,128)S(1)}, f32[40,128]{1,0:T(8,128)S(1)}, u32[]{:S(2)}, u32[]{:S(2)}) collective-permute-start(f32[40,128]{1,0:T(8,128)S(1)} %copy-done.11), channel_id=1, source_target_pairs={{1,0},{2,1},{3,2},{5,4},{6,5},{7,6},{9,8},{10,9},{11,10},{13,12},{... | collective-permute-start | bytes 61448 | tf_op jit(solution)/shard_map/ppermute | solution.py:277
  62.6 5.8 %collective-permute-start.24 = (f32[56,128]{1,0:T(8,128)S(1)}, f32[56,128]{1,0:T(8,128)S(1)}, u32[]{:S(2)}, u32[]{:S(2)}) collective-permute-start(f32[56,128]{1,0:T(8,128)S(1)} %copy-done.9), channel_id=1, source_target_pairs={{0,1},{1,2},{2,3},{4,5},{5,6},{6,7},{8,9},{9,10},{10,11},{12,13},{... | collective-permute-start | bytes 86024 | tf_op jit(solution)/shard_map/ppermute | solution.py:277
  63.9 4.5 %copy-start.4 = (f32[64,128]{1,0:T(8,128)S(1)}, f32[64,128]{1,0:T(8,128)}, u32[]{:S(2)}) copy-start(f32[64,128]{1,0:T(8,128)} %area.3) | copy-start | bytes 98308
  68.4 23.8 %collective-permute-start.11 = (f32[56,128]{1,0:T(8,128)S(1)}, f32[56,128]{1,0:T(8,128)}, u32[]{:S(2)}, u32[]{:S(2)}) collective-permute-start(f32[56,128]{1,0:T(8,128)S(1)} %get-tuple-element.737), channel_id=1, source_target_pairs={{3,135},{7,131},{11,127},{15,123},{19,119},{23,115},{27,111},{31,1... | collective-permute-start | bytes 86024 | tf_op jit(solution)/shard_map/cond/branch_11_fun/ppermute | solution.py:292
  93.1 1.5 %copy-start.7 = (f32[16,64,128]{2,1,0:T(8,128)}, f32[16,64,128]{2,1,0:T(8,128)S(1)}, u32[]{:S(2)}) copy-start(f32[16,64,128]{2,1,0:T(8,128)S(1)} %get-tuple-element.917) | copy-start | bytes 1572868
  94.6 0.8 copy-start.6
where the time goes:
time: 96.6 us; the launch traced here: 95.3 us
  starting transfers between devices  75.4 us (78%)
  Pallas kernels  9.49 us (10%)
  waiting for transfers between devices  6.67 us (7%)
  local copies, waits for them, and re-layouts  2.11 us (2%)
  between operations  1.05 us (1%)
    all_to_all x2, starting transfers between devices, all_sum(): return jnp.sum(lax.all_to_all(copies, axes, 0, 0, tiled=True), axis=0)  47.9 us
    ppermute x1, starting transfers between devices, branch(): return (lax.ppermute(rows, GX + ('gy',), pairs), beside(*arrays))  18.7 us
    ppermute x4, starting transfers between devices, along(): return lax.ppermute(block, axis, pairs)  8.73 us
    ppermute x4, waiting for transfers between devices, along(): return lax.ppermute(block, axis, pairs)  4.42 us
    pallas_call x1, Pallas kernels, packs(): pl.pallas_call(pack_kernel, in_specs=[VMEM] * 5, out_specs=[VMEM] * 5, ou...  3.43 us
    pallas_call x1, Pallas kernels, tracer_step(): pl.pallas_call(step_kernel, in_specs=[VMEM] * 12, out_specs=[VMEM] * 2, o...  2.85 us
    ppermute x1, waiting for transfers between devices, branch(): return (lax.ppermute(rows, GX + ('gy',), pairs), beside(*arrays))  2.24 us
  transfers between devices with their start and end apart: 7, of which 3 were waited for; matrix products, arithmetic and copies ran while one was open for 1% of the time, Pallas kernels for 7%

commit v1 on v0

--- a/solution.py
+++ b/solution.py
@@ -5,6 +5,7 @@
 from jax.experimental.pallas import tpu as pltpu
 from jax.sharding import Mesh
 from jax.sharding import PartitionSpec as P
+
 
 time_step = 0.25
 diffusivity = 0.5
@@ -123,7 +124,7 @@
 
 def step_kernel(
     heat, salt, currents, sea, layers, area,
-    west_own, east_own, west_halo, east_halo, south_halo, north_halo,
+    west_own, east_own, west_halo, east_halo,
     heat_out, salt_out,
 ):
     levels, rows, _ = heat.shape
@@ -131,13 +132,9 @@
     lane = lane_of((rows, LANES))
     row = lax.broadcasted_iota(jnp.int32, (rows, LANES), 0)
     first_lane, last_lane = lane == 0, lane == LANES - 1
-    first_row, last_row = row == 0, row == rows - 1
+    last_row = row == rows - 1
     depth = (sea[...] * layers[...]).astype(jnp.float32)
-    base = 2 * levels
-    south_depth = south_halo[base : base + 1]
-    depth_north = jnp.where(last_row, north_halo[base : base + 1], pltpu.roll(depth, rows - 1, 0))
-    open_north = jnp.minimum(depth, depth_north)
-    open_south = jnp.minimum(depth[0:1], south_depth)
+    open_north = jnp.where(last_row, 0.0, jnp.minimum(depth, pltpu.roll(depth, rows - 1, 0)))
     open_east = jnp.where(last_lane, 0.0, jnp.minimum(depth, pltpu.roll(depth, LANES - 1, 1)))
     per_area = time_step / area[...]
     edge_level = (lane_of((8, LANES)) // blocks).astype(jnp.float32)
@@ -155,7 +152,6 @@
     def one_level(k, above):
         level = k.astype(jnp.float32)
         east_speed, north_speed = currents[0, k], currents[1, k]
-        south_speed = south_halo[pl.ds(base + 8 + k, 1)]
         east_up, east_down = jnp.maximum(east_speed, 0.0), jnp.minimum(east_speed, 0.0)
         north_up, north_down = jnp.maximum(north_speed, 0.0), jnp.minimum(north_speed, 0.0)
         east_wet = level < open_east
@@ -165,7 +161,6 @@
         passed = []
         for f in range(2):
             cells = fields[f][k]
-            at = f * levels + k
             east_flux = jnp.where(
                 east_wet, open_flux(cells, pltpu.roll(cells, LANES - 1, 1), east_up, east_down), 0.0
             )
@@ -177,12 +172,9 @@
                 east_columns.append(pltpu.roll(east_edge[f], LANES - 1 - place, 1))
             west_flux = jnp.where(first_lane, jnp.concatenate(west_columns, axis=0), west_flux)
             east_flux = jnp.where(last_lane, jnp.concatenate(east_columns, axis=0), east_flux)
-            northern = jnp.where(last_row, north_halo[pl.ds(at, 1)], pltpu.roll(cells, rows - 1, 0))
+            northern = pltpu.roll(cells, rows - 1, 0)
             north_flux = jnp.where(north_wet, open_flux(cells, northern, north_up, north_down), 0.0)
-            first_flux = edge_flux(
-                south_halo[pl.ds(at, 1)], cells[0:1], south_speed, open_south, open_south, level
-            )
-            south_flux = jnp.where(first_row, first_flux, pltpu.roll(north_flux, 1, 0))
+            south_flux = pltpu.roll(north_flux, 1, 0)
             next_cells = fields[f][jnp.minimum(k + 1, levels - 1)]
             below = jnp.where(below_wet, vertical_mixing * (cells - next_cells), 0.0)
             change = per_area * (west_flux - east_flux + south_flux - north_flux) + time_step * (above[f] - below)
@@ -198,50 +190,78 @@
     heat = arrays[0]
     return pl.pallas_call(
         step_kernel,
-        in_specs=[VMEM] * 12,
+        in_specs=[VMEM] * 10,
         out_specs=[VMEM] * 2,
         out_shape=[jax.ShapeDtypeStruct(heat.shape, jnp.float32)] * 2,
         name="tracer_step",
     )(*arrays)
 
 
-def fold_kernel(heat_next, salt_next, own, fold, area, heat_out, salt_out):
+def edge_kernel(
+    flags, heat_next, salt_next, south_own, north_own, south_halo, north_halo, fold_halo, area, heat_out, salt_out
+):
     levels, band, _ = heat_next.shape
     base = 2 * levels
     level = lax.broadcasted_iota(jnp.int32, (levels, LANES), 0).astype(jnp.float32)
-    per_area = time_step / area[band - 1 : band]
-    speed = 0.5 * (own[base + 8 :] - fold[base + 8 :])
-    last = lax.broadcasted_iota(jnp.int32, (band, LANES), 0) == band - 1
-    for f, (before, after) in enumerate(((heat_next, heat_out), (salt_next, salt_out))):
-        flux = edge_flux(
-            own[f * levels : f * levels + levels], fold[f * levels : f * levels + levels], speed,
-            own[base : base + 1], fold[base : base + 1], level,
-        )
-        leaving = per_area * flux
-        for k in range(levels):
-            after[k] = before[k] - jnp.where(last, leaving[k : k + 1], 0.0)
-
-
-def close_fold(heat_next, salt_next, own, fold, area):
+    row = lax.broadcasted_iota(jnp.int32, (band, LANES), 0)
+    is_top = flags[0] == 1
+    fields = ((heat_next, heat_out), (salt_next, salt_out))
+
+    def cells(rows, f):
+        return rows[f * levels : f * levels + levels]
+
+    @pl.when(pl.program_id(0) == 0)
+    def _():
+        for f, (before, after) in enumerate(fields):
+            flux = edge_flux(
+                cells(south_halo, f), cells(south_own, f), south_halo[base + 8 :],
+                south_halo[base : base + 1], south_own[base : base + 1], level,
+            )
+            entering = time_step / area[0:1] * flux
+            for k in range(levels):
+                after[k] = before[k] + jnp.where(row == 0, entering[k : k + 1], 0.0)
+
+    @pl.when(pl.program_id(0) == 1)
+    def _():
+        speed = north_own[base + 8 :]
+        speed = jnp.where(is_top, 0.5 * (speed - fold_halo[base + 8 :]), speed)
+        far_depth = jnp.where(is_top, fold_halo[base : base + 1], north_halo[base : base + 1])
+        for f, (before, after) in enumerate(fields):
+            far = jnp.where(is_top, cells(fold_halo, f), cells(north_halo, f))
+            flux = edge_flux(cells(north_own, f), far, speed, north_own[base : base + 1], far_depth, level)
+            leaving = time_step / area[band - 1 : band] * flux
+            for k in range(levels):
+                after[k] = before[k] - jnp.where(row == band - 1, leaving[k : k + 1], 0.0)
+
+
+def close_edges(is_top, heat_next, salt_next, south_own, north_own, south_halo, north_halo, fold_halo, area):
     levels, rows, width = heat_next.shape
-    band = pl.BlockSpec((levels, 8, width), lambda i: (0, rows // 8 - 1, 0))
-    whole = pl.BlockSpec(own.shape, lambda i: (0, 0))
-    return pl.pallas_call(
-        fold_kernel,
-        grid=(1,),
-        in_specs=[band, band, whole, whole, pl.BlockSpec((8, width), lambda i: (rows // 8 - 1, 0))],
+    gap = rows // 8 - 1
+    band = pl.BlockSpec((levels, 8, width), lambda i: (0, i * gap, 0))
+
+    def whole(rows):
+        return pl.BlockSpec(rows.shape, lambda i: (0, 0))
+
+    packs = (south_own, north_own, south_halo, north_halo, fold_halo)
+    return pl.pallas_call(
+        edge_kernel,
+        grid=(2,),
+        in_specs=[pl.BlockSpec(memory_space=pltpu.SMEM), band, band]
+        + [whole(rows) for rows in packs]
+        + [pl.BlockSpec((8, width), lambda i: (i * gap, 0))],
         out_specs=[band, band],
         out_shape=[jax.ShapeDtypeStruct(heat_next.shape, jnp.float32)] * 2,
-        input_output_aliases={0: 0, 1: 1},
-        name="close_fold",
-    )(heat_next, salt_next, own, fold, area)
+        input_output_aliases={1: 0, 2: 1},
+        name="close_edges",
+    )(is_top, heat_next, salt_next, *packs, area)
 
 
 def final_kernel(salt_next, surface, rain, sea, totals, out):
     lane = lane_of((1, LANES))
+    summed = jnp.sum(totals[...], axis=0)
 
     def total(place):
-        return jnp.sum(jnp.where(lane == place, totals[...], 0.0), axis=1, keepdims=True)
+        return jnp.sum(jnp.where(lane == place, summed, 0.0), axis=1, keepdims=True)
 
     total_area, total_fresh, salt_fresh, salt_only = (total(place) for place in range(4))
     mean_fresh = total_fresh / total_area
@@ -259,7 +279,7 @@
     return pl.pallas_call(
         final_kernel,
         grid=(1,),
-        in_specs=[top, top, plane, plane, pl.BlockSpec((1, LANES), lambda i: (0, 0))],
+        in_specs=[top, top, plane, plane, pl.BlockSpec(totals.shape, lambda i: (0, 0, 0))],
         out_specs=top,
         out_shape=jax.ShapeDtypeStruct(salt_next.shape, jnp.float32),
         input_output_aliases={0: 0},
@@ -267,8 +287,8 @@
     )(salt_next, brine, rain, sea, totals)
 
 
-def all_sum(copies, axes):
-    return jnp.sum(lax.all_to_all(copies, axes, 0, 0, tiled=True), axis=0)
+def share(copies, axes):
+    return lax.all_to_all(copies, axes, 0, 0, tiled=True)
 
 
 def along(block, axis, by, closed):
@@ -299,23 +319,21 @@
 def shards(heat, brine, currents, sea, layers, area, rain, seam):
     _, _, width = heat.shape
     sums = local_sums(brine, sea, area, rain, lax.axis_size(NEAR))
-    plane = all_sum(sums, NEAR)
+    plane = jnp.sum(share(sums, NEAR), axis=0)
+    totals = share(jnp.broadcast_to(plane[None], (lax.axis_size("chip"),) + plane.shape), "chip")
     west_own, east_own, south_own, north_own, fold_own = packs(heat, brine, currents, sea, layers)
-    plane, west_own, east_own, south_own, north_own = lax.optimization_barrier(
-        (plane, west_own, east_own, south_own, north_own)
-    )
-    totals = all_sum(jnp.broadcast_to(plane[None], (lax.axis_size("chip"),) + plane.shape), "chip")
     west_halo = along(east_own, GX, 1, True)
     east_halo = along(west_own, GX, -1, True)
-    south_halo = along(north_own, "gy", 1, False)
-    north_halo = along(south_own, "gy", -1, False)
     place, branches, held = fold_exchange(fold_own, west_halo[32:], east_halo[24:], seam, width, tracer_step)
-    arrays = (
-        heat, brine, currents, sea, layers, area,
-        west_own, east_own, west_halo, east_halo, south_halo, north_halo,
+    arrays = (heat, brine, currents, sea, layers, area, west_own, east_own, west_halo, east_halo)
+    fold_halo, (heat_next, salt_next) = lax.switch(place, branches, held, arrays)
+    north_sent, south_sent, fold_halo = lax.optimization_barrier((north_own, south_own, fold_halo))
+    south_halo = along(north_sent, "gy", 1, False)
+    north_halo = along(south_sent, "gy", -1, False)
+    is_top = (lax.axis_index("gy") == lax.axis_size("gy") - 1).astype(jnp.int32)
+    heat_next, salt_next = close_edges(
+        is_top[None], heat_next, salt_next, south_own, north_own, south_halo, north_halo, fold_halo, area
     )
-    fold_halo, (heat_next, salt_next) = lax.switch(place, branches, held, arrays)
-    heat_next, salt_next = close_fold(heat_next, salt_next, north_own, fold_halo, area)
     return heat_next, add_virtual(salt_next, brine, rain, sea, totals)
 
 

time: 96.6 us -> 100 us (1.035)
  the two profiles are of different devices: /device:TPU:38 before, /device:TPU:44 now
where the time goes in v1:
time: 100 us; the launch traced here: 99.8 us
  starting transfers between devices  79.1 us (79%)
  Pallas kernels  9.78 us (10%)
  waiting for transfers between devices  5.64 us (6%)
  local copies, waits for them, and re-layouts  4.09 us (4%)
  between operations  1.06 us (1%)
    ppermute x4, starting transfers between devices, along(): return lax.ppermute(block, axis, pairs)  68.2 us
    all_to_all x2, starting transfers between devices, share(): return lax.all_to_all(copies, axes, 0, 0, tiled=True)  9.53 us
    ppermute x4, waiting for transfers between devices, along(): return lax.ppermute(block, axis, pairs)  3.75 us
    pallas_call x1, Pallas kernels, packs(): pl.pallas_call(pack_kernel, in_specs=[VMEM] * 5, out_specs=[VMEM] * 5, ou...  3.6 us
    unnamed x30, local copies, waits for them, and re-layouts  3.48 us
    pallas_call x1, Pallas kernels, tracer_step(): pl.pallas_call(step_kernel, in_specs=[VMEM] * 10, out_specs=[VMEM] * 2, o...  2.84 us
  transfers between devices with their start and end apart: 7, of which 2 were waited for; matrix products, arithmetic and copies ran while one was open for 1% of the time, Pallas kernels for 5%

profile of v1, /device:TPU:44, one launch (start us, length us, event | category | flops | bytes accessed | tf_op | source)
XLA Modules:
  0.0 99.8 jit_solution(14423284443004203407)
XLA Ops:
  0.6 0.0 copy-start.1
  0.6 0.0 copy-start
  0.7 0.0 copy-start.3
  0.7 0.0 copy-start.4
  0.7 3.6 %edge_packs.1 = (f32[80,128]{1,0:T(8,128)S(1)}, f32[88,128]{1,0:T(8,128)S(1)}, f32[40,128]{1,0:T(8,128)}, f32[56,128]{1,0:T(8,128)}, f32[56,128]{1,0:T(8,128)}) custom-call(f32[16,64,128]{2,1,0:T(8,128)} %heat.1, f32[16,64,128]{2,1,0:T(8,128)} %surface.3, f32[2,16,64,128]{3,2,1,0:T(8,128)} %currents.1, s32[64,128]{1,0:T(8,128)} %sea.5, s32[64,128]{1,0:T(8,128)} %layers.1), custom_call_target="tpu_custom_call" | custom-call | tf_op jit(solution)/shard_map/edge_packs/pallas_call | solution.py:107
  4.3 0.0 copy-start.2
  4.3 0.0 collective-permute-start.22
  4.3 42.9 %collective-permute-start.23 = (f32[80,128]{1,0:T(8,128)S(1)}, f32[80,128]{1,0:T(8,128)S(1)}, u32[]{:S(2)}, u32[]{:S(2)}) collective-permute-start(f32[80,128]{1,0:T(8,128)S(1)} %get-tuple-element.786), channel_id=1, source_target_pairs={{0,252},{4,0},{8,4},{12,8},{16,12},{20,16},{24,20},{28,24},{32,28}... | collective-permute-start | bytes 122888 | tf_op jit(solution)/shard_map/ppermute | solution.py:297
  47.2 0.0 copy-done.1
  47.2 0.0 copy-done.3
  47.2 0.0 copy-done.4
  47.2 1.5 %local_sums.1 = f32[8,1,128]{2,1,0:T(1,128)} custom-call(f32[16,64,128]{2,1,0:T(8,128)S(1)} %copy-done.1, s32[64,128]{1,0:T(8,128)S(1)} %copy-done.3, f32[64,128]{1,0:T(8,128)S(1)} %copy-done.4, f32[64,128]{1,0:T(8,128)} %rain.3), custom_call_target="tpu_custom_call" | custom-call | tf_op jit(solution)/shard_map/local_sums/pallas_call | solution.py:41
  48.7 4.8 %all-to-all-start = ((f32[8,1,128]{2,1,0:T(1,128)}), f32[8,1,128]{2,1,0:T(1,128)S(1)}, u32[]{:S(2)}, u32[]{:S(2)}) async-start(f32[8,1,128]{2,1,0:T(1,128)} %local_sums.1), calls=%async_computation | async-start | bytes 8192 | tf_op jit(solution)/shard_map/all_to_all | solution.py:291
  53.5 0.0 copy-start.14
  53.5 0.7 copy-done.14
  54.3 0.0 copy-start.9
  54.4 1.9 %all-to-all-done = f32[8,1,128]{2,1,0:T(1,128)S(1)} async-done(((f32[8,1,128]{2,1,0:T(1,128)}), f32[8,1,128]{2,1,0:T(1,128)S(1)}, u32[]{:S(2)}, u32[]{:S(2)}) %all-to-all-start) | async-done | bytes 4128 | tf_op jit(solution)/shard_map/all_to_all | solution.py:291
  56.3 0.6 broadcast_in_dim.13
  56.9 4.7 %all-to-all-start.1 = ((f32[32,1,128]{2,1,0:T(1,128)}), f32[32,1,128]{2,1,0:T(1,128)S(1)}, u32[]{:S(2)}, u32[]{:S(2)}) async-start(f32[32,1,128]{2,1,0:T(1,128)} %broadcast_in_dim.13), calls=%async_computation.1 | async-start | bytes 32768 | tf_op jit(solution)/shard_map/all_to_all | solution.py:291
  61.6 0.0 collective-permute-done.23
  61.6 0.0 collective-permute-done.22
  61.6 0.0 copy-done.9
  61.6 0.0 copy-start.5
  61.7 0.0 copy-done
  61.7 0.0 copy-done.2
  61.7 0.7 copy-done.5
  62.4 0.0 copy-start.10
  62.4 4.3 %conditional.1 = (f32[56,128]{1,0:T(8,128)}, f32[16,64,128]{2,1,0:T(8,128)S(1)}, f32[16,64,128]{2,1,0:T(8,128)S(1)}) conditional(s32[]{:T(128)} %clamp.3, (f32[56,128]{1,0:T(8,128)S(1)}, f32[16,64,128]{2,1,0:T(8,128)S(1)}, f32[16,64,128]{2,1,0:T(8,128)S(1)}, f32[2,16,64,128]{3,2,1,0:T(8,128)S(1)}, ...), branch_computations={%region_0.0_spmd, %region_1.2_spmd, %region_2.3_spmd, %region_3.4_... | conditional | bytes 114752 | solution.py:329
  62.4 1.4 %collective-permute-start.11 = (f32[56,128]{1,0:T(8,128)S(1)}, f32[56,128]{1,0:T(8,128)}, u32[]{:S(2)}, u32[]{:S(2)}) collective-permute-start(f32[56,128]{1,0:T(8,128)S(1)} %get-tuple-element.627), channel_id=1, source_target_pairs={{3,135},{7,131},{11,127},{15,123},{19,119},{23,115},{27,111},{31,1... | collective-permute-start | bytes 86024 | tf_op jit(solution)/shard_map/cond/branch_11_fun/ppermute | solution.py:312
  63.8 2.8 %tracer_step.33 = (f32[16,64,128]{2,1,0:T(8,128)S(1)}, f32[16,64,128]{2,1,0:T(8,128)S(1)}) custom-call(f32[16,64,128]{2,1,0:T(8,128)S(1)} %get-tuple-element.628.heat, f32[16,64,128]{2,1,0:T(8,128)S(1)} %get-tuple-element.629.salt, f32[2,16,64,128]{3,2,1,0:T(8,128)S(1)} %get-tuple-element.630.currents, s32[64,128]{1,0:T(8,128)S(1)} %get-tuple-element.631.sea, ...), custom_call_target="tpu_custom_call" | custom-call | tf_op jit(solution)/shard_map/cond/branch_11_fun/tracer_step/pallas_call | solution.py:191
  66.6 0.0 collective-permute-done.11
  66.7 0.0 copy-done.10
  66.7 23.4 %collective-permute-start.24 = (f32[56,128]{1,0:T(8,128)S(1)}, f32[56,128]{1,0:T(8,128)S(1)}, u32[]{:S(2)}, u32[]{:S(2)}) collective-permute-start(f32[56,128]{1,0:T(8,128)S(1)} %copy-done.10), channel_id=1, source_target_pairs={{0,1},{1,2},{2,3},{4,5},{5,6},{6,7},{8,9},{9,10},{10,11},{12,13},{... | collective-permute-start | bytes 86024 | tf_op jit(solution)/shard_map/ppermute | solution.py:297
  90.0 0.0 copy-done.12
  90.1 2.0 %collective-permute-start.25 = (f32[40,128]{1,0:T(8,128)S(1)}, f32[40,128]{1,0:T(8,128)S(1)}, u32[]{:S(2)}, u32[]{:S(2)}) collective-permute-start(f32[40,128]{1,0:T(8,128)S(1)} %copy-done.12), channel_id=1, source_target_pairs={{1,0},{2,1},{3,2},{5,4},{6,5},{7,6},{9,8},{10,9},{11,10},{13,12},{... | collective-permute-start | bytes 61448 | tf_op jit(solution)/shard_map/ppermute | solution.py:297
  92.0 3.7 %collective-permute-done.25.north_halo = f32[40,128]{1,0:T(8,128)S(1)} collective-permute-done((f32[40,128]{1,0:T(8,128)S(1)}, f32[40,128]{1,0:T(8,128)S(1)}, u32[]{:S(2)}, u32[]{:S(2)}) %collective-permute-start.25) | collective-permute-done | bytes 20512 | tf_op jit(solution)/shard_map/ppermute | solution.py:297
  95.8 0.0 collective-permute-done.24.south_halo
  95.8 0.6 copy-done.13
  96.4 0.0 copy-done.11
  96.4 1.0 %close_edges.1 = (f32[16,64,128]{2,1,0:T(8,128)S(1)}, f32[16,64,128]{2,1,0:T(8,128)S(1)}) custom-call(s32[1]{0:T(128)} %bitcast.flags, f32[16,64,128]{2,1,0:T(8,128)S(1)} %get-tuple-element.788.heat_next, f32[16,64,128]{2,1,0:T(8,128)S(1)} %get-tuple-element.789.salt_next, ...), custom_call_target="tpu_custom_call", output_to_operand_aliasing={{0}: (1, {}), {1}: (2, {})} | custom-call | tf_op jit(solution)/shard_map/close_edges/pallas_call | solution.py:246
  97.4 0.0 copy-start.7
  97.4 0.0 all-to-all-done.1.totals
  97.4 0.0 copy-start.8
  97.4 0.7 copy-done.8
  98.1 0.9 add_virtual.1
  99.0 0.0 copy-done.7
  99.0 0.0 copy-start.6
  99.0 0.8 copy-done.6
  (5 shorter events, 0.0 us)
Async XLA Ops:
  0.6 46.6 %copy-start.1 = (f32[16,64,128]{2,1,0:T(8,128)S(1)}, f32[16,64,128]{2,1,0:T(8,128)}, u32[]{:S(2)}) copy-start(f32[16,64,128]{2,1,0:T(8,128)} %surface.3) | copy-start | bytes 1572868
  0.6 61.0 %copy-start = (f32[2,16,64,128]{3,2,1,0:T(8,128)S(1)}, f32[2,16,64,128]{3,2,1,0:T(8,128)}, u32[]{:S(2)}) copy-start(f32[2,16,64,128]{3,2,1,0:T(8,128)} %currents.1) | copy-start | bytes 3145732
  0.7 46.6 %copy-start.3 = (s32[64,128]{1,0:T(8,128)S(1)}, s32[64,128]{1,0:T(8,128)}, u32[]{:S(2)}) copy-start(s32[64,128]{1,0:T(8,128)} %sea.5) | copy-start | bytes 98308
  0.7 46.5 %copy-start.4 = (f32[64,128]{1,0:T(8,128)S(1)}, f32[64,128]{1,0:T(8,128)}, u32[]{:S(2)}) copy-start(f32[64,128]{1,0:T(8,128)} %area.3) | copy-start | bytes 98308
  4.3 57.4 %copy-start.2 = (f32[16,64,128]{2,1,0:T(8,128)S(1)}, f32[16,64,128]{2,1,0:T(8,128)}, u32[]{:S(2)}) copy-start(f32[16,64,128]{2,1,0:T(8,128)} %heat.1) | copy-start | bytes 1572868
  4.3 57.3 %collective-permute-start.22 = (f32[88,128]{1,0:T(8,128)S(1)}, f32[88,128]{1,0:T(8,128)S(1)}, u32[]{:S(2)}, u32[]{:S(2)}) collective-permute-start(f32[88,128]{1,0:T(8,128)S(1)} %get-tuple-element.785), channel_id=1, source_target_pairs={{0,4},{4,8},{8,12},{12,16},{16,20},{20,24},{24,28},{28,32},{32,36}... | collective-permute-start | bytes 135176 | tf_op jit(solution)/shard_map/ppermute | solution.py:297
  4.3 57.3 %collective-permute-start.23 = (f32[80,128]{1,0:T(8,128)S(1)}, f32[80,128]{1,0:T(8,128)S(1)}, u32[]{:S(2)}, u32[]{:S(2)}) collective-permute-start(f32[80,128]{1,0:T(8,128)S(1)} %get-tuple-element.786), channel_id=1, source_target_pairs={{0,252},{4,0},{8,4},{12,8},{16,12},{20,16},{24,20},{28,24},{32,28}... | collective-permute-start | bytes 122888 | tf_op jit(solution)/shard_map/ppermute | solution.py:297
  48.7 7.6 %all-to-all-start = ((f32[8,1,128]{2,1,0:T(1,128)}), f32[8,1,128]{2,1,0:T(1,128)S(1)}, u32[]{:S(2)}, u32[]{:S(2)}) async-start(f32[8,1,128]{2,1,0:T(1,128)} %local_sums.1), calls=%async_computation | async-start | bytes 8192 | tf_op jit(solution)/shard_map/all_to_all | solution.py:291
  53.5 0.7 copy-start.14
  54.3 7.3 %copy-start.9 = (f32[56,128]{1,0:T(8,128)S(1)}, f32[56,128]{1,0:T(8,128)}, u32[]{:S(2)}) copy-start(f32[56,128]{1,0:T(8,128)} %get-tuple-element.787) | copy-start | bytes 86020
  56.9 40.5 %all-to-all-start.1 = ((f32[32,1,128]{2,1,0:T(1,128)}), f32[32,1,128]{2,1,0:T(1,128)S(1)}, u32[]{:S(2)}, u32[]{:S(2)}) async-start(f32[32,1,128]{2,1,0:T(1,128)} %broadcast_in_dim.13), calls=%async_computation.1 | async-start | bytes 32768 | tf_op jit(solution)/shard_map/all_to_all | solution.py:291
  61.6 0.8 copy-start.5
  62.4 4.3 %copy-start.10 = (f32[56,128]{1,0:T(8,128)S(1)}, f32[56,128]{1,0:T(8,128)}, u32[]{:S(2)}) copy-start(f32[56,128]{1,0:T(8,128)} %get-tuple-element.793.north_own) | copy-start | bytes 86020
  62.4 27.6 %copy-start.12 = (f32[40,128]{1,0:T(8,128)S(1)}, f32[40,128]{1,0:T(8,128)}, u32[]{:S(2)}) copy-start(f32[40,128]{1,0:T(8,128)} %get-tuple-element.794.south_own) | copy-start | bytes 61444
  62.4 4.2 %collective-permute-start.11 = (f32[56,128]{1,0:T(8,128)S(1)}, f32[56,128]{1,0:T(8,128)}, u32[]{:S(2)}, u32[]{:S(2)}) collective-permute-start(f32[56,128]{1,0:T(8,128)S(1)} %get-tuple-element.627), channel_id=1, source_target_pairs={{3,135},{7,131},{11,127},{15,123},{19,119},{23,115},{27,111},{31,1... | collective-permute-start | bytes 86024 | tf_op jit(solution)/shard_map/cond/branch_11_fun/ppermute | solution.py:312
  66.7 29.1 %collective-permute-start.24 = (f32[56,128]{1,0:T(8,128)S(1)}, f32[56,128]{1,0:T(8,128)S(1)}, u32[]{:S(2)}, u32[]{:S(2)}) collective-permute-start(f32[56,128]{1,0:T(8,128)S(1)} %copy-done.10), channel_id=1, source_target_pairs={{0,1},{1,2},{2,3},{4,5},{5,6},{6,7},{8,9},{9,10},{10,11},{12,13},{... | collective-permute-start | bytes 86024 | tf_op jit(solution)/shard_map/ppermute | solution.py:297
  90.1 5.7 %collective-permute-start.25 = (f32[40,128]{1,0:T(8,128)S(1)}, f32[40,128]{1,0:T(8,128)S(1)}, u32[]{:S(2)}, u32[]{:S(2)}) collective-permute-start(f32[40,128]{1,0:T(8,128)S(1)} %copy-done.12), channel_id=1, source_target_pairs={{1,0},{2,1},{3,2},{5,4},{6,5},{7,6},{9,8},{10,9},{11,10},{13,12},{... | collective-permute-start | bytes 61448 | tf_op jit(solution)/shard_map/ppermute | solution.py:297
  95.8 0.6 copy-start.13
  95.8 0.6 copy-start.11
  97.4 1.6 %copy-start.7 = (f32[16,64,128]{2,1,0:T(8,128)}, f32[16,64,128]{2,1,0:T(8,128)S(1)}, u32[]{:S(2)}) copy-start(f32[16,64,128]{2,1,0:T(8,128)S(1)} %get-tuple-element.783) | copy-start | bytes 1572868
  97.4 0.7 copy-start.8
  99.0 0.8 copy-start.6

commit v2 on v0

--- a/solution.py
+++ b/solution.py
@@ -5,6 +5,7 @@
 from jax.experimental.pallas import tpu as pltpu
 from jax.sharding import Mesh
 from jax.sharding import PartitionSpec as P
+
 
 time_step = 0.25
 diffusivity = 0.5
@@ -267,8 +268,8 @@
     )(salt_next, brine, rain, sea, totals)
 
 
-def all_sum(copies, axes):
-    return jnp.sum(lax.all_to_all(copies, axes, 0, 0, tiled=True), axis=0)
+def share(copies, axes):
+    return lax.all_to_all(copies, axes, 0, 0, tiled=True)
 
 
 def along(block, axis, by, closed):
@@ -277,44 +278,42 @@
     return lax.ppermute(block, axis, pairs)
 
 
-def fold_exchange(own, from_west, from_east, seam, width, beside):
+def fold_branches(beside):
     around, height = lax.axis_size(GX), lax.axis_size("gy")
-    centre = (seam[0] // width + lax.axis_index(GX)) % around
-    part = (centre + 1) % 3
-    held = jnp.where(part == 0, from_west, jnp.where(part == 2, from_east, own))
 
     def mirror(coarse):
         pairs = [
             (i * height + height - 1, (3 * coarse - i) % around * height + height - 1) for i in range(around)
         ]
 
-        def branch(rows, arrays):
-            return lax.ppermute(rows, GX + ("gy",), pairs), beside(*arrays)
+        def branch(rows, arrays, south_own, north_own):
+            fold_halo = lax.ppermute(rows, GX + ("gy",), pairs)
+            south_halo = along(north_own, "gy", 1, False)
+            north_halo = along(south_own, "gy", -1, False)
+            return fold_halo, beside(*arrays, south_halo, north_halo)
 
         return branch
 
-    return (centre + 1) // 3, [mirror(coarse) for coarse in range((around + 2) // 3)], held
+    return [mirror(coarse) for coarse in range((around + 2) // 3)]
 
 
 def shards(heat, brine, currents, sea, layers, area, rain, seam):
     _, _, width = heat.shape
     sums = local_sums(brine, sea, area, rain, lax.axis_size(NEAR))
-    plane = all_sum(sums, NEAR)
+    plane = jnp.sum(share(sums, NEAR), axis=0)
+    centre = (seam[0] // width + lax.axis_index(GX)) % lax.axis_size(GX)
+    place, part = (centre + 1) // 3, (centre + 1) % 3
+    layers, place, part = lax.optimization_barrier((layers, place, part))
     west_own, east_own, south_own, north_own, fold_own = packs(heat, brine, currents, sea, layers)
-    plane, west_own, east_own, south_own, north_own = lax.optimization_barrier(
-        (plane, west_own, east_own, south_own, north_own)
-    )
-    totals = all_sum(jnp.broadcast_to(plane[None], (lax.axis_size("chip"),) + plane.shape), "chip")
+    totals = share(jnp.broadcast_to(plane[None], (lax.axis_size("chip"),) + plane.shape), "chip")
+    totals = jnp.sum(totals, axis=0)
     west_halo = along(east_own, GX, 1, True)
     east_halo = along(west_own, GX, -1, True)
-    south_halo = along(north_own, "gy", 1, False)
-    north_halo = along(south_own, "gy", -1, False)
-    place, branches, held = fold_exchange(fold_own, west_halo[32:], east_halo[24:], seam, width, tracer_step)
-    arrays = (
-        heat, brine, currents, sea, layers, area,
-        west_own, east_own, west_halo, east_halo, south_halo, north_halo,
+    held = jnp.where(part == 0, west_halo[32:], jnp.where(part == 2, east_halo[24:], fold_own))
+    arrays = (heat, brine, currents, sea, layers, area, west_own, east_own, west_halo, east_halo)
+    fold_halo, (heat_next, salt_next) = lax.switch(
+        place, fold_branches(tracer_step), held, arrays, south_own, north_own
     )
-    fold_halo, (heat_next, salt_next) = lax.switch(place, branches, held, arrays)
     heat_next, salt_next = close_fold(heat_next, salt_next, north_own, fold_halo, area)
     return heat_next, add_virtual(salt_next, brine, rain, sea, totals)
 

time: 96.6 us -> 98 us (1.014)
  the two profiles are of different devices: /device:TPU:38 before, /device:TPU:45 now
where the time goes in v2:
time: 98 us; the launch traced here: 97.4 us
  starting transfers between devices  59.3 us (61%)
  waiting for transfers between devices  22.8 us (23%)
  Pallas kernels  10.3 us (11%)
  local copies, waits for them, and re-layouts  3.4 us (3%)
  between operations  0.98 us (1%)
    all_to_all x2, starting transfers between devices, share(): return lax.all_to_all(copies, axes, 0, 0, tiled=True)  49.7 us
    ppermute x4, waiting for transfers between devices, along(): return lax.ppermute(block, axis, pairs)  20.2 us
    ppermute x4, starting transfers between devices, along(): return lax.ppermute(block, axis, pairs)  8.32 us
    pallas_call x1, Pallas kernels, packs(): pl.pallas_call(pack_kernel, in_specs=[VMEM] * 5, out_specs=[VMEM] * 5, ou...  3.6 us
    pallas_call x1, Pallas kernels, tracer_step(): pl.pallas_call(step_kernel, in_specs=[VMEM] * 12, out_specs=[VMEM] * 2, o...  3.57 us
    all_to_all x2, waiting for transfers between devices, share(): return lax.all_to_all(copies, axes, 0, 0, tiled=True)  2.55 us
    unnamed x20, local copies, waits for them, and re-layouts  2.17 us
  transfers between devices with their start and end apart: 7, of which 2 were waited for; matrix products, arithmetic and copies ran while one was open for 1% of the time, Pallas kernels for 6%

profile of v2, /device:TPU:45, one launch (start us, length us, event | category | flops | bytes accessed | tf_op | source)
XLA Modules:
  0.0 97.4 jit_solution(8594856588437795719)
XLA Ops:
  0.6 0.0 copy-start.53
  0.6 0.6 copy-done.53
  1.4 0.0 copy-start.5
  1.5 0.0 copy-start.3
  1.5 0.7 copy-done.5
  2.2 0.0 copy-done.3
  2.2 0.0 copy-start.1
  2.2 0.0 copy-start.4
  2.2 0.0 copy-start
  2.2 3.6 %edge_packs.1 = (f32[80,128]{1,0:T(8,128)S(1)}, f32[88,128]{1,0:T(8,128)S(1)}, f32[40,128]{1,0:T(8,128)S(1)}, f32[56,128]{1,0:T(8,128)S(1)}, f32[56,128]{1,0:T(8,128)}) custom-call(f32[16,64,128]{2,1,0:T(8,128)} %heat.1, f32[16,64,128]{2,1,0:T(8,128)} %surface.3, f32[2,16,64,128]{3,2,1,0:T(8,128)} %currents.1, s32[64,128]{1,0:T(8,128)S(1)} %copy-done.3, ...), custom_call_target="tpu_custom_call" | custom-call | tf_op jit(solution)/shard_map/edge_packs/pallas_call | solution.py:107
  5.8 0.0 copy-start.2
  5.8 3.0 %collective-permute-start.66 = (f32[88,128]{1,0:T(8,128)S(1)}, f32[88,128]{1,0:T(8,128)S(1)}, u32[]{:S(2)}, u32[]{:S(2)}) collective-permute-start(f32[88,128]{1,0:T(8,128)S(1)} %get-tuple-element.920), channel_id=1, source_target_pairs={{0,4},{4,8},{8,12},{12,16},{16,20},{20,24},{24,28},{28,32},{32,36}... | collective-permute-start | bytes 135176 | tf_op jit(solution)/shard_map/ppermute | solution.py:278
  8.8 0.0 collective-permute-start.67
  8.8 0.0 copy-done.1
  8.8 0.0 copy-done.4
  8.8 1.5 %local_sums.1 = f32[8,1,128]{2,1,0:T(1,128)} custom-call(f32[16,64,128]{2,1,0:T(8,128)S(1)} %copy-done.1, s32[64,128]{1,0:T(8,128)S(1)} %copy-done.3, f32[64,128]{1,0:T(8,128)S(1)} %copy-done.4, f32[64,128]{1,0:T(8,128)} %rain.3), custom_call_target="tpu_custom_call" | custom-call | tf_op jit(solution)/shard_map/local_sums/pallas_call | solution.py:41
  10.3 44.9 %all-to-all-start = ((f32[8,1,128]{2,1,0:T(1,128)}), f32[8,1,128]{2,1,0:T(1,128)S(1)}, u32[]{:S(2)}, u32[]{:S(2)}) async-start(f32[8,1,128]{2,1,0:T(1,128)} %local_sums.1), calls=%async_computation | async-start | bytes 8192 | tf_op jit(solution)/shard_map/all_to_all | solution.py:272
  55.2 0.0 copy-start.30
  55.2 2.5 %all-to-all-done = f32[8,1,128]{2,1,0:T(1,128)S(1)} async-done(((f32[8,1,128]{2,1,0:T(1,128)}), f32[8,1,128]{2,1,0:T(1,128)S(1)}, u32[]{:S(2)}, u32[]{:S(2)}) %all-to-all-start) | async-done | bytes 4128 | tf_op jit(solution)/shard_map/all_to_all | solution.py:272
  57.8 0.6 broadcast_in_dim.2
  58.4 4.8 %all-to-all-start.1 = ((f32[32,1,128]{2,1,0:T(1,128)}), f32[32,1,128]{2,1,0:T(1,128)S(1)}, u32[]{:S(2)}, u32[]{:S(2)}) async-start(f32[32,1,128]{2,1,0:T(1,128)} %broadcast_in_dim.2), calls=%async_computation.1 | async-start | bytes 32768 | tf_op jit(solution)/shard_map/all_to_all | solution.py:272
  63.2 0.0 collective-permute-done.67
  63.2 0.0 collective-permute-done.66
  63.2 0.0 copy-done.30
  63.2 0.0 copy-done
  63.2 0.0 copy-done.2
  63.3 31.1 %conditional.1 = (f32[56,128]{1,0:T(8,128)}, f32[16,64,128]{2,1,0:T(8,128)S(1)}, f32[16,64,128]{2,1,0:T(8,128)S(1)}) conditional(s32[]{:T(128)} %clamp.3, (f32[56,128]{1,0:T(8,128)S(1)}, f32[56,128]{1,0:T(8,128)S(1)}, f32[40,128]{1,0:T(8,128)S(1)}, f32[16,64,128]{2,1,0:T(8,128)S(1)}, f32[16,64,128]{2,1,0:T(8,128)S(1)}, ...), branch_computations={%region_0.0_spmd, %region_1.2_spmd, %region_2.3_spmd, %region_3.4_... | conditional | bytes 508104 | solution.py:314
  63.3 3.1 %collective-permute-start.34 = (f32[56,128]{1,0:T(8,128)S(1)}, f32[56,128]{1,0:T(8,128)S(1)}, u32[]{:S(2)}, u32[]{:S(2)}) collective-permute-start(f32[56,128]{1,0:T(8,128)S(1)} %get-tuple-element.748), channel_id=1, source_target_pairs={{0,1},{1,2},{2,3},{4,5},{5,6},{6,7},{8,9},{9,10},{10,11},{12,13},{... | collective-permute-start | bytes 86024 | tf_op jit(solution)/shard_map/cond/branch_11_fun/ppermute | solution.py:278
  66.4 1.3 %collective-permute-start.33 = (f32[56,128]{1,0:T(8,128)S(1)}, f32[56,128]{1,0:T(8,128)}, u32[]{:S(2)}, u32[]{:S(2)}) collective-permute-start(f32[56,128]{1,0:T(8,128)S(1)} %get-tuple-element.737), channel_id=1, source_target_pairs={{3,135},{7,131},{11,127},{15,123},{19,119},{23,115},{27,111},{31,1... | collective-permute-start | bytes 86024 | tf_op jit(solution)/shard_map/cond/branch_11_fun/ppermute | solution.py:290
  67.7 2.2 %collective-permute-start.35 = (f32[40,128]{1,0:T(8,128)S(1)}, f32[40,128]{1,0:T(8,128)S(1)}, u32[]{:S(2)}, u32[]{:S(2)}) collective-permute-start(f32[40,128]{1,0:T(8,128)S(1)} %get-tuple-element.749), channel_id=1, source_target_pairs={{1,0},{2,1},{3,2},{5,4},{6,5},{7,6},{9,8},{10,9},{11,10},{13,12},{... | collective-permute-start | bytes 61448 | tf_op jit(solution)/shard_map/cond/branch_11_fun/ppermute | solution.py:278
  69.9 20.2 %collective-permute-done.35.north_halo = f32[40,128]{1,0:T(8,128)S(1)} collective-permute-done((f32[40,128]{1,0:T(8,128)S(1)}, f32[40,128]{1,0:T(8,128)S(1)}, u32[]{:S(2)}, u32[]{:S(2)}) %collective-permute-start.35) | collective-permute-done | bytes 20512 | tf_op jit(solution)/shard_map/cond/branch_11_fun/ppermute | solution.py:278
  90.1 0.0 copy-start.42
  90.1 0.0 collective-permute-done.34.south_halo
  90.1 0.0 copy-start.19
  90.1 0.6 copy-done.42
  90.7 0.0 copy-done.19
  90.8 3.6 %tracer_step.33 = (f32[16,64,128]{2,1,0:T(8,128)S(1)}, f32[16,64,128]{2,1,0:T(8,128)S(1)}) custom-call(f32[16,64,128]{2,1,0:T(8,128)S(1)} %get-tuple-element.738.heat, f32[16,64,128]{2,1,0:T(8,128)S(1)} %get-tuple-element.739.salt, f32[2,16,64,128]{3,2,1,0:T(8,128)S(1)} %get-tuple-element.740.currents, s32[64,128]{1,0:T(8,128)S(1)} %get-tuple-element.741.sea, ...), custom_call_target="tpu_custom_call" | custom-call | tf_op jit(solution)/shard_map/cond/branch_11_fun/tracer_step/pallas_call | solution.py:200
  94.3 0.0 collective-permute-done.33
  94.4 0.8 close_fold.1
  95.2 0.0 copy-start.7
  95.2 0.0 all-to-all-done.1
  95.2 0.6 reduce_sum.21
  95.8 0.9 add_virtual.1
  96.6 0.0 copy-done.7
  96.6 0.0 copy-start.6
  96.6 0.8 copy-done.6
  (2 shorter events, 0.0 us)
Async XLA Ops:
  0.6 0.7 copy-start.53
  1.4 0.8 copy-start.5
  1.5 0.8 copy-start.3
  2.2 6.6 %copy-start.1 = (f32[16,64,128]{2,1,0:T(8,128)S(1)}, f32[16,64,128]{2,1,0:T(8,128)}, u32[]{:S(2)}) copy-start(f32[16,64,128]{2,1,0:T(8,128)} %surface.3) | copy-start | bytes 1572868
  2.2 6.6 %copy-start.4 = (f32[64,128]{1,0:T(8,128)S(1)}, f32[64,128]{1,0:T(8,128)}, u32[]{:S(2)}) copy-start(f32[64,128]{1,0:T(8,128)} %area.3) | copy-start | bytes 98308
  2.2 61.0 %copy-start = (f32[2,16,64,128]{3,2,1,0:T(8,128)S(1)}, f32[2,16,64,128]{3,2,1,0:T(8,128)}, u32[]{:S(2)}) copy-start(f32[2,16,64,128]{3,2,1,0:T(8,128)} %currents.1) | copy-start | bytes 3145732
  5.8 57.4 %copy-start.2 = (f32[16,64,128]{2,1,0:T(8,128)S(1)}, f32[16,64,128]{2,1,0:T(8,128)}, u32[]{:S(2)}) copy-start(f32[16,64,128]{2,1,0:T(8,128)} %heat.1) | copy-start | bytes 1572868
  5.8 57.4 %collective-permute-start.66 = (f32[88,128]{1,0:T(8,128)S(1)}, f32[88,128]{1,0:T(8,128)S(1)}, u32[]{:S(2)}, u32[]{:S(2)}) collective-permute-start(f32[88,128]{1,0:T(8,128)S(1)} %get-tuple-element.920), channel_id=1, source_target_pairs={{0,4},{4,8},{8,12},{12,16},{16,20},{20,24},{24,28},{28,32},{32,36}... | collective-permute-start | bytes 135176 | tf_op jit(solution)/shard_map/ppermute | solution.py:278
  8.8 54.4 %collective-permute-start.67 = (f32[80,128]{1,0:T(8,128)S(1)}, f32[80,128]{1,0:T(8,128)S(1)}, u32[]{:S(2)}, u32[]{:S(2)}) collective-permute-start(f32[80,128]{1,0:T(8,128)S(1)} %get-tuple-element.921), channel_id=1, source_target_pairs={{0,252},{4,0},{8,4},{12,8},{16,12},{20,16},{24,20},{28,24},{32,28}... | collective-permute-start | bytes 122888 | tf_op jit(solution)/shard_map/ppermute | solution.py:278
  10.3 47.5 %all-to-all-start = ((f32[8,1,128]{2,1,0:T(1,128)}), f32[8,1,128]{2,1,0:T(1,128)S(1)}, u32[]{:S(2)}, u32[]{:S(2)}) async-start(f32[8,1,128]{2,1,0:T(1,128)} %local_sums.1), calls=%async_computation | async-start | bytes 8192 | tf_op jit(solution)/shard_map/all_to_all | solution.py:272
  55.2 8.0 %copy-start.30 = (f32[56,128]{1,0:T(8,128)S(1)}, f32[56,128]{1,0:T(8,128)}, u32[]{:S(2)}) copy-start(f32[56,128]{1,0:T(8,128)} %get-tuple-element.922) | copy-start | bytes 86020
  58.4 36.8 %all-to-all-start.1 = ((f32[32,1,128]{2,1,0:T(1,128)}), f32[32,1,128]{2,1,0:T(1,128)S(1)}, u32[]{:S(2)}, u32[]{:S(2)}) async-start(f32[32,1,128]{2,1,0:T(1,128)} %broadcast_in_dim.2), calls=%async_computation.1 | async-start | bytes 32768 | tf_op jit(solution)/shard_map/all_to_all | solution.py:272
  63.3 26.8 %collective-permute-start.34 = (f32[56,128]{1,0:T(8,128)S(1)}, f32[56,128]{1,0:T(8,128)S(1)}, u32[]{:S(2)}, u32[]{:S(2)}) collective-permute-start(f32[56,128]{1,0:T(8,128)S(1)} %get-tuple-element.748), channel_id=1, source_target_pairs={{0,1},{1,2},{2,3},{4,5},{5,6},{6,7},{8,9},{9,10},{10,11},{12,13},{... | collective-permute-start | bytes 86024 | tf_op jit(solution)/shard_map/cond/branch_11_fun/ppermute | solution.py:278
  66.4 27.9 %collective-permute-start.33 = (f32[56,128]{1,0:T(8,128)S(1)}, f32[56,128]{1,0:T(8,128)}, u32[]{:S(2)}, u32[]{:S(2)}) collective-permute-start(f32[56,128]{1,0:T(8,128)S(1)} %get-tuple-element.737), channel_id=1, source_target_pairs={{3,135},{7,131},{11,127},{15,123},{19,119},{23,115},{27,111},{31,1... | collective-permute-start | bytes 86024 | tf_op jit(solution)/shard_map/cond/branch_11_fun/ppermute | solution.py:290
  67.7 22.4 %collective-permute-start.35 = (f32[40,128]{1,0:T(8,128)S(1)}, f32[40,128]{1,0:T(8,128)S(1)}, u32[]{:S(2)}, u32[]{:S(2)}) collective-permute-start(f32[40,128]{1,0:T(8,128)S(1)} %get-tuple-element.749), channel_id=1, source_target_pairs={{1,0},{2,1},{3,2},{5,4},{6,5},{7,6},{9,8},{10,9},{11,10},{13,12},{... | collective-permute-start | bytes 61448 | tf_op jit(solution)/shard_map/cond/branch_11_fun/ppermute | solution.py:278
  90.1 0.6 copy-start.42
  90.1 0.6 copy-start.19
  95.2 1.5 %copy-start.7 = (f32[16,64,128]{2,1,0:T(8,128)}, f32[16,64,128]{2,1,0:T(8,128)S(1)}, u32[]{:S(2)}) copy-start(f32[16,64,128]{2,1,0:T(8,128)S(1)} %get-tuple-element.915) | copy-start | bytes 1572868
  96.6 0.8 copy-start.6

commit v3 on v2

--- a/solution.py
+++ b/solution.py
@@ -94,16 +94,20 @@
         north[2 * levels + 8 + k : 2 * levels + 9 + k] = currents[1, k, last:rows]
     south[2 * levels : 2 * levels + 8] = jnp.broadcast_to(depth[0:1], (8, LANES))
     north[2 * levels : 2 * levels + 8] = jnp.broadcast_to(depth[last:rows], (8, LANES))
-    turned = mirrored(north[...])
-    fold[...] = turned
-    west[24:] = turned
-    east[32:] = turned
+    level = lax.broadcasted_iota(jnp.int32, (levels, LANES), 0).astype(jnp.float32)
+    fold[0:levels] = mirrored(north[0:levels])
+    fold[levels : 2 * levels] = mirrored(
+        jnp.where(level < depth[last:rows], north[levels : 2 * levels], 0.0)
+    )
+    fold[2 * levels :] = mirrored(north[2 * levels + 8 :])
+    west[24:] = fold[...]
+    east[32:] = fold[...]
 
 
 def packs(heat, salt, currents, sea, layers):
     levels, _, _ = heat.shape
     north = 3 * levels + 8
-    shapes = (24 + north, 32 + north, 2 * levels + 8, north, north)
+    shapes = (24 + 3 * levels, 32 + 3 * levels, 2 * levels + 8, north, 3 * levels)
     return pl.pallas_call(
         pack_kernel,
         in_specs=[VMEM] * 5,
@@ -211,26 +215,26 @@
     base = 2 * levels
     level = lax.broadcasted_iota(jnp.int32, (levels, LANES), 0).astype(jnp.float32)
     per_area = time_step / area[band - 1 : band]
-    speed = 0.5 * (own[base + 8 :] - fold[base + 8 :])
+    speed = 0.5 * (own[base + 8 :] - fold[base:])
     last = lax.broadcasted_iota(jnp.int32, (band, LANES), 0) == band - 1
+    wet = jnp.logical_and(level < own[base : base + 1], fold[levels:base] > 0.0)
+    forward, backward = jnp.maximum(speed, 0.0), jnp.minimum(speed, 0.0)
     for f, (before, after) in enumerate(((heat_next, heat_out), (salt_next, salt_out))):
-        flux = edge_flux(
-            own[f * levels : f * levels + levels], fold[f * levels : f * levels + levels], speed,
-            own[base : base + 1], fold[base : base + 1], level,
-        )
+        near, far = own[f * levels : f * levels + levels], fold[f * levels : f * levels + levels]
+        flux = jnp.where(wet, open_flux(near, far, forward, backward), 0.0)
         leaving = per_area * flux
         for k in range(levels):
             after[k] = before[k] - jnp.where(last, leaving[k : k + 1], 0.0)
 
 
 def close_fold(heat_next, salt_next, own, fold, area):
-    levels, rows, width = heat_next.shape
-    band = pl.BlockSpec((levels, 8, width), lambda i: (0, rows // 8 - 1, 0))
-    whole = pl.BlockSpec(own.shape, lambda i: (0, 0))
+    levels, height, width = heat_next.shape
+    band = pl.BlockSpec((levels, 8, width), lambda i: (0, height // 8 - 1, 0))
+    own_rows, fold_rows = (pl.BlockSpec(rows.shape, lambda i: (0, 0)) for rows in (own, fold))
     return pl.pallas_call(
         fold_kernel,
         grid=(1,),
-        in_specs=[band, band, whole, whole, pl.BlockSpec((8, width), lambda i: (rows // 8 - 1, 0))],
+        in_specs=[band, band, own_rows, fold_rows, pl.BlockSpec((8, width), lambda i: (height // 8 - 1, 0))],
         out_specs=[band, band],
         out_shape=[jax.ShapeDtypeStruct(heat_next.shape, jnp.float32)] * 2,
         input_output_aliases={0: 0, 1: 1},
@@ -286,11 +290,8 @@
             (i * height + height - 1, (3 * coarse - i) % around * height + height - 1) for i in range(around)
         ]
 
-        def branch(rows, arrays, south_own, north_own):
-            fold_halo = lax.ppermute(rows, GX + ("gy",), pairs)
-            south_halo = along(north_own, "gy", 1, False)
-            north_halo = along(south_own, "gy", -1, False)
-            return fold_halo, beside(*arrays, south_halo, north_halo)
+        def branch(rows, arrays):
+            return lax.ppermute(rows, GX + ("gy",), pairs), beside(*arrays)
 
         return branch
 
@@ -309,11 +310,14 @@
     totals = jnp.sum(totals, axis=0)
     west_halo = along(east_own, GX, 1, True)
     east_halo = along(west_own, GX, -1, True)
+    north_halo = along(south_own, "gy", -1, False)
+    south_halo = along(north_own, "gy", 1, False)
     held = jnp.where(part == 0, west_halo[32:], jnp.where(part == 2, east_halo[24:], fold_own))
-    arrays = (heat, brine, currents, sea, layers, area, west_own, east_own, west_halo, east_halo)
-    fold_halo, (heat_next, salt_next) = lax.switch(
-        place, fold_branches(tracer_step), held, arrays, south_own, north_own
+    arrays = (
+        heat, brine, currents, sea, layers, area,
+        west_own, east_own, west_halo, east_halo, south_halo, north_halo,
     )
+    fold_halo, (heat_next, salt_next) = lax.switch(place, fold_branches(tracer_step), held, arrays)
     heat_next, salt_next = close_fold(heat_next, salt_next, north_own, fold_halo, area)
     return heat_next, add_virtual(salt_next, brine, rain, sea, totals)
 

time: 98 us -> 94.6 us (0.965)
  the two profiles are of different devices: /device:TPU:45 before, /device:TPU:38 now
where the time goes in v3:
time: 94.6 us; the launch traced here: 93 us
  starting transfers between devices  78.6 us (83%)
  Pallas kernels  9.53 us (10%)
  local copies, waits for them, and re-layouts  2.79 us (3%)
  between operations  1.05 us (1%)
    ppermute x4, starting transfers between devices, along(): return lax.ppermute(block, axis, pairs)  48.8 us
    ppermute x1, starting transfers between devices, branch(): return (lax.ppermute(rows, GX + ('gy',), pairs), beside(*arrays))  20.4 us
    all_to_all x2, starting transfers between devices, share(): return lax.all_to_all(copies, axes, 0, 0, tiled=True)  9.31 us
    pallas_call x1, Pallas kernels, packs(): pl.pallas_call(pack_kernel, in_specs=[VMEM] * 5, out_specs=[VMEM] * 5, ou...  3.54 us
    pallas_call x1, Pallas kernels, tracer_step(): pl.pallas_call(step_kernel, in_specs=[VMEM] * 12, out_specs=[VMEM] * 2, o...  2.9 us
    unnamed x24, local copies, waits for them, and re-layouts  2.18 us
  transfers between devices with their start and end apart: 7, of which 1 were waited for; matrix products, arithmetic and copies ran while one was open for 1% of the time, Pallas kernels for 6%

profile of v3, /device:TPU:38, one launch (start us, length us, event | category | flops | bytes accessed | tf_op | source)
XLA Modules:
  0.0 93.0 jit_solution(848261384441846541)
XLA Ops:
  0.6 0.0 copy-start.10
  0.6 0.6 copy-done.10
  1.4 0.0 copy-start.5
  1.5 0.0 copy-start.3
  1.5 0.7 copy-done.5
  2.2 0.0 copy-done.3
  2.2 0.0 copy-start.1
  2.2 0.0 copy-start.4
  2.2 0.0 copy-start
  2.2 3.5 %edge_packs.1 = (f32[72,128]{1,0:T(8,128)S(1)}, f32[80,128]{1,0:T(8,128)S(1)}, f32[40,128]{1,0:T(8,128)}, f32[56,128]{1,0:T(8,128)}, f32[48,128]{1,0:T(8,128)}) custom-call(f32[16,64,128]{2,1,0:T(8,128)} %heat.1, f32[16,64,128]{2,1,0:T(8,128)} %surface.3, f32[2,16,64,128]{3,2,1,0:T(8,128)} %currents.1, s32[64,128]{1,0:T(8,128)S(1)} %copy-done.3, ...), custom_call_target="tpu_custom_call" | custom-call | tf_op jit(solution)/shard_map/edge_packs/pallas_call | solution.py:111
  5.8 0.0 copy-start.2
  5.8 0.0 collective-permute-start.22
  5.8 0.0 copy-start.8
  5.8 0.0 copy-start.11
  5.8 43.0 %collective-permute-start.23 = (f32[72,128]{1,0:T(8,128)S(1)}, f32[72,128]{1,0:T(8,128)S(1)}, u32[]{:S(2)}, u32[]{:S(2)}) collective-permute-start(f32[72,128]{1,0:T(8,128)S(1)} %get-tuple-element.921), channel_id=1, source_target_pairs={{0,252},{4,0},{8,4},{12,8},{16,12},{20,16},{24,20},{28,24},{32,28}... | collective-permute-start | bytes 110600 | tf_op jit(solution)/shard_map/ppermute | solution.py:282
  48.7 0.0 copy-done.1
  48.7 0.0 copy-done.4
  48.7 1.4 %local_sums.1 = f32[8,1,128]{2,1,0:T(1,128)} custom-call(f32[16,64,128]{2,1,0:T(8,128)S(1)} %copy-done.1, s32[64,128]{1,0:T(8,128)S(1)} %copy-done.3, f32[64,128]{1,0:T(8,128)S(1)} %copy-done.4, f32[64,128]{1,0:T(8,128)} %rain.3), custom_call_target="tpu_custom_call" | custom-call | tf_op jit(solution)/shard_map/local_sums/pallas_call | solution.py:41
  50.2 4.7 %all-to-all-start = ((f32[8,1,128]{2,1,0:T(1,128)}), f32[8,1,128]{2,1,0:T(1,128)S(1)}, u32[]{:S(2)}, u32[]{:S(2)}) async-start(f32[8,1,128]{2,1,0:T(1,128)} %local_sums.1), calls=%async_computation | async-start | bytes 8192 | tf_op jit(solution)/shard_map/all_to_all | solution.py:276
  54.8 0.0 copy-done.8
  54.8 1.3 %collective-permute-start.24 = (f32[56,128]{1,0:T(8,128)S(1)}, f32[56,128]{1,0:T(8,128)S(1)}, u32[]{:S(2)}, u32[]{:S(2)}) collective-permute-start(f32[56,128]{1,0:T(8,128)S(1)} %copy-done.8), channel_id=1, source_target_pairs={{0,1},{1,2},{2,3},{4,5},{5,6},{6,7},{8,9},{9,10},{10,11},{12,13},{... | collective-permute-start | bytes 86024 | tf_op jit(solution)/shard_map/ppermute | solution.py:282
  56.2 0.0 copy-done.11
  56.2 4.6 %collective-permute-start.25 = (f32[40,128]{1,0:T(8,128)S(1)}, f32[40,128]{1,0:T(8,128)S(1)}, u32[]{:S(2)}, u32[]{:S(2)}) collective-permute-start(f32[40,128]{1,0:T(8,128)S(1)} %copy-done.11), channel_id=1, source_target_pairs={{1,0},{2,1},{3,2},{5,4},{6,5},{7,6},{9,8},{10,9},{11,10},{13,12},{... | collective-permute-start | bytes 61448 | tf_op jit(solution)/shard_map/ppermute | solution.py:282
  60.8 0.0 all-to-all-done
  60.8 0.0 copy-start.9
  60.8 0.6 broadcast_in_dim.2
  61.4 4.7 %all-to-all-start.1 = ((f32[32,1,128]{2,1,0:T(1,128)}), f32[32,1,128]{2,1,0:T(1,128)S(1)}, u32[]{:S(2)}, u32[]{:S(2)}) async-start(f32[32,1,128]{2,1,0:T(1,128)} %broadcast_in_dim.2), calls=%async_computation.1 | async-start | bytes 32768 | tf_op jit(solution)/shard_map/all_to_all | solution.py:276
  66.1 0.0 collective-permute-done.23
  66.1 0.0 collective-permute-done.22
  66.1 0.0 copy-done.9
  66.1 0.0 collective-permute-done.25
  66.2 0.0 collective-permute-done.24
  66.2 0.0 copy-done
  66.2 0.0 copy-done.2
  66.2 23.8 %conditional.1 = (f32[48,128]{1,0:T(8,128)}, f32[16,64,128]{2,1,0:T(8,128)S(1)}, f32[16,64,128]{2,1,0:T(8,128)S(1)}) conditional(s32[]{:T(128)} %clamp.3, (f32[48,128]{1,0:T(8,128)S(1)}, f32[16,64,128]{2,1,0:T(8,128)S(1)}, f32[16,64,128]{2,1,0:T(8,128)S(1)}, f32[2,16,64,128]{3,2,1,0:T(8,128)S(1)}, ...), branch_computations={%region_0.0_spmd, %region_1.2_spmd, %region_2.3_spmd, %region_3.4_... | conditional | bytes 98368 | solution.py:320
  66.2 20.4 %collective-permute-start.11 = (f32[48,128]{1,0:T(8,128)S(1)}, f32[48,128]{1,0:T(8,128)}, u32[]{:S(2)}, u32[]{:S(2)}) collective-permute-start(f32[48,128]{1,0:T(8,128)S(1)} %get-tuple-element.737), channel_id=1, source_target_pairs={{3,135},{7,131},{11,127},{15,123},{19,119},{23,115},{27,111},{31,1... | collective-permute-start | bytes 73736 | tf_op jit(solution)/shard_map/cond/branch_11_fun/ppermute | solution.py:294
  86.7 2.9 %tracer_step.33 = (f32[16,64,128]{2,1,0:T(8,128)S(1)}, f32[16,64,128]{2,1,0:T(8,128)S(1)}) custom-call(f32[16,64,128]{2,1,0:T(8,128)S(1)} %get-tuple-element.738.heat, f32[16,64,128]{2,1,0:T(8,128)S(1)} %get-tuple-element.739.salt, f32[2,16,64,128]{3,2,1,0:T(8,128)S(1)} %get-tuple-element.740.currents, s32[64,128]{1,0:T(8,128)S(1)} %get-tuple-element.741.sea, ...), custom_call_target="tpu_custom_call" | custom-call | tf_op jit(solution)/shard_map/cond/branch_11_fun/tracer_step/pallas_call | solution.py:204
  89.6 0.4 collective-permute-done.11
  89.9 0.8 close_fold.1
  90.8 0.0 copy-start.7
  90.8 0.0 all-to-all-done.1
  90.8 0.6 reduce_sum.21
  91.4 0.9 add_virtual.1
  92.2 0.0 copy-done.7
  92.2 0.0 copy-start.6
  92.2 0.8 copy-done.6
  (2 shorter events, 0.0 us)
Async XLA Ops:
  0.6 0.7 copy-start.10
  1.4 0.8 copy-start.5
  1.5 0.8 copy-start.3
  2.2 46.5 %copy-start.1 = (f32[16,64,128]{2,1,0:T(8,128)S(1)}, f32[16,64,128]{2,1,0:T(8,128)}, u32[]{:S(2)}) copy-start(f32[16,64,128]{2,1,0:T(8,128)} %surface.3) | copy-start | bytes 1572868
  2.2 46.5 %copy-start.4 = (f32[64,128]{1,0:T(8,128)S(1)}, f32[64,128]{1,0:T(8,128)}, u32[]{:S(2)}) copy-start(f32[64,128]{1,0:T(8,128)} %area.3) | copy-start | bytes 98308
  2.2 63.9 %copy-start = (f32[2,16,64,128]{3,2,1,0:T(8,128)S(1)}, f32[2,16,64,128]{3,2,1,0:T(8,128)}, u32[]{:S(2)}) copy-start(f32[2,16,64,128]{3,2,1,0:T(8,128)} %currents.1) | copy-start | bytes 3145732
  5.8 60.4 %copy-start.2 = (f32[16,64,128]{2,1,0:T(8,128)S(1)}, f32[16,64,128]{2,1,0:T(8,128)}, u32[]{:S(2)}) copy-start(f32[16,64,128]{2,1,0:T(8,128)} %heat.1) | copy-start | bytes 1572868
  5.8 60.3 %collective-permute-start.22 = (f32[80,128]{1,0:T(8,128)S(1)}, f32[80,128]{1,0:T(8,128)S(1)}, u32[]{:S(2)}, u32[]{:S(2)}) collective-permute-start(f32[80,128]{1,0:T(8,128)S(1)} %get-tuple-element.920), channel_id=1, source_target_pairs={{0,4},{4,8},{8,12},{12,16},{16,20},{20,24},{24,28},{28,32},{32,36}... | collective-permute-start | bytes 122888 | tf_op jit(solution)/shard_map/ppermute | solution.py:282
  5.8 49.1 %copy-start.8 = (f32[56,128]{1,0:T(8,128)S(1)}, f32[56,128]{1,0:T(8,128)}, u32[]{:S(2)}) copy-start(f32[56,128]{1,0:T(8,128)} %get-tuple-element.923.own) | copy-start | bytes 86020
  5.8 50.4 %copy-start.11 = (f32[40,128]{1,0:T(8,128)S(1)}, f32[40,128]{1,0:T(8,128)}, u32[]{:S(2)}) copy-start(f32[40,128]{1,0:T(8,128)} %get-tuple-element.924) | copy-start | bytes 61444
  5.8 60.3 %collective-permute-start.23 = (f32[72,128]{1,0:T(8,128)S(1)}, f32[72,128]{1,0:T(8,128)S(1)}, u32[]{:S(2)}, u32[]{:S(2)}) collective-permute-start(f32[72,128]{1,0:T(8,128)S(1)} %get-tuple-element.921), channel_id=1, source_target_pairs={{0,252},{4,0},{8,4},{12,8},{16,12},{20,16},{24,20},{28,24},{32,28}... | collective-permute-start | bytes 110600 | tf_op jit(solution)/shard_map/ppermute | solution.py:282
  50.2 10.6 %all-to-all-start = ((f32[8,1,128]{2,1,0:T(1,128)}), f32[8,1,128]{2,1,0:T(1,128)S(1)}, u32[]{:S(2)}, u32[]{:S(2)}) async-start(f32[8,1,128]{2,1,0:T(1,128)} %local_sums.1), calls=%async_computation | async-start | bytes 8192 | tf_op jit(solution)/shard_map/all_to_all | solution.py:276
  54.8 11.3 %collective-permute-start.24 = (f32[56,128]{1,0:T(8,128)S(1)}, f32[56,128]{1,0:T(8,128)S(1)}, u32[]{:S(2)}, u32[]{:S(2)}) collective-permute-start(f32[56,128]{1,0:T(8,128)S(1)} %copy-done.8), channel_id=1, source_target_pairs={{0,1},{1,2},{2,3},{4,5},{5,6},{6,7},{8,9},{9,10},{10,11},{12,13},{... | collective-permute-start | bytes 86024 | tf_op jit(solution)/shard_map/ppermute | solution.py:282
  56.2 10.0 %collective-permute-start.25 = (f32[40,128]{1,0:T(8,128)S(1)}, f32[40,128]{1,0:T(8,128)S(1)}, u32[]{:S(2)}, u32[]{:S(2)}) collective-permute-start(f32[40,128]{1,0:T(8,128)S(1)} %copy-done.11), channel_id=1, source_target_pairs={{1,0},{2,1},{3,2},{5,4},{6,5},{7,6},{9,8},{10,9},{11,10},{13,12},{... | collective-permute-start | bytes 61448 | tf_op jit(solution)/shard_map/ppermute | solution.py:282
  60.8 5.3 %copy-start.9 = (f32[48,128]{1,0:T(8,128)S(1)}, f32[48,128]{1,0:T(8,128)}, u32[]{:S(2)}) copy-start(f32[48,128]{1,0:T(8,128)} %get-tuple-element.922) | copy-start | bytes 73732
  61.4 29.3 %all-to-all-start.1 = ((f32[32,1,128]{2,1,0:T(1,128)}), f32[32,1,128]{2,1,0:T(1,128)S(1)}, u32[]{:S(2)}, u32[]{:S(2)}) async-start(f32[32,1,128]{2,1,0:T(1,128)} %broadcast_in_dim.2), calls=%async_computation.1 | async-start | bytes 32768 | tf_op jit(solution)/shard_map/all_to_all | solution.py:276
  66.2 23.7 %collective-permute-start.11 = (f32[48,128]{1,0:T(8,128)S(1)}, f32[48,128]{1,0:T(8,128)}, u32[]{:S(2)}, u32[]{:S(2)}) collective-permute-start(f32[48,128]{1,0:T(8,128)S(1)} %get-tuple-element.737), channel_id=1, source_target_pairs={{3,135},{7,131},{11,127},{15,123},{19,119},{23,115},{27,111},{31,1... | collective-permute-start | bytes 73736 | tf_op jit(solution)/shard_map/cond/branch_11_fun/ppermute | solution.py:294
  90.8 1.5 %copy-start.7 = (f32[16,64,128]{2,1,0:T(8,128)}, f32[16,64,128]{2,1,0:T(8,128)S(1)}, u32[]{:S(2)}) copy-start(f32[16,64,128]{2,1,0:T(8,128)S(1)} %get-tuple-element.915) | copy-start | bytes 1572868
  92.2 0.8 copy-start.6

commit v4 on v3

--- a/solution.py
+++ b/solution.py
@@ -128,7 +128,7 @@
 
 def step_kernel(
     heat, salt, currents, sea, layers, area,
-    west_own, east_own, west_halo, east_halo, south_halo, north_halo,
+    west_own, east_own, west_halo, east_halo, north_halo,
     heat_out, salt_out,
 ):
     levels, rows, _ = heat.shape
@@ -139,10 +139,8 @@
     first_row, last_row = row == 0, row == rows - 1
     depth = (sea[...] * layers[...]).astype(jnp.float32)
     base = 2 * levels
-    south_depth = south_halo[base : base + 1]
     depth_north = jnp.where(last_row, north_halo[base : base + 1], pltpu.roll(depth, rows - 1, 0))
     open_north = jnp.minimum(depth, depth_north)
-    open_south = jnp.minimum(depth[0:1], south_depth)
     open_east = jnp.where(last_lane, 0.0, jnp.minimum(depth, pltpu.roll(depth, LANES - 1, 1)))
     per_area = time_step / area[...]
     edge_level = (lane_of((8, LANES)) // blocks).astype(jnp.float32)
@@ -160,7 +158,6 @@
     def one_level(k, above):
         level = k.astype(jnp.float32)
         east_speed, north_speed = currents[0, k], currents[1, k]
-        south_speed = south_halo[pl.ds(base + 8 + k, 1)]
         east_up, east_down = jnp.maximum(east_speed, 0.0), jnp.minimum(east_speed, 0.0)
         north_up, north_down = jnp.maximum(north_speed, 0.0), jnp.minimum(north_speed, 0.0)
         east_wet = level < open_east
@@ -184,10 +181,7 @@
             east_flux = jnp.where(last_lane, jnp.concatenate(east_columns, axis=0), east_flux)
             northern = jnp.where(last_row, north_halo[pl.ds(at, 1)], pltpu.roll(cells, rows - 1, 0))
             north_flux = jnp.where(north_wet, open_flux(cells, northern, north_up, north_down), 0.0)
-            first_flux = edge_flux(
-                south_halo[pl.ds(at, 1)], cells[0:1], south_speed, open_south, open_south, level
-            )
-            south_flux = jnp.where(first_row, first_flux, pltpu.roll(north_flux, 1, 0))
+            south_flux = jnp.where(first_row, 0.0, pltpu.roll(north_flux, 1, 0))
             next_cells = fields[f][jnp.minimum(k + 1, levels - 1)]
             below = jnp.where(below_wet, vertical_mixing * (cells - next_cells), 0.0)
             change = per_area * (west_flux - east_flux + south_flux - north_flux) + time_step * (above[f] - below)
@@ -203,43 +197,62 @@
     heat = arrays[0]
     return pl.pallas_call(
         step_kernel,
-        in_specs=[VMEM] * 12,
+        in_specs=[VMEM] * 11,
         out_specs=[VMEM] * 2,
         out_shape=[jax.ShapeDtypeStruct(heat.shape, jnp.float32)] * 2,
         name="tracer_step",
     )(*arrays)
 
 
-def fold_kernel(heat_next, salt_next, own, fold, area, heat_out, salt_out):
+def close_kernel(heat_next, salt_next, south_own, north_own, south_halo, fold, area, heat_out, salt_out):
     levels, band, _ = heat_next.shape
     base = 2 * levels
     level = lax.broadcasted_iota(jnp.int32, (levels, LANES), 0).astype(jnp.float32)
-    per_area = time_step / area[band - 1 : band]
-    speed = 0.5 * (own[base + 8 :] - fold[base:])
-    last = lax.broadcasted_iota(jnp.int32, (band, LANES), 0) == band - 1
-    wet = jnp.logical_and(level < own[base : base + 1], fold[levels:base] > 0.0)
-    forward, backward = jnp.maximum(speed, 0.0), jnp.minimum(speed, 0.0)
-    for f, (before, after) in enumerate(((heat_next, heat_out), (salt_next, salt_out))):
-        near, far = own[f * levels : f * levels + levels], fold[f * levels : f * levels + levels]
-        flux = jnp.where(wet, open_flux(near, far, forward, backward), 0.0)
-        leaving = per_area * flux
-        for k in range(levels):
-            after[k] = before[k] - jnp.where(last, leaving[k : k + 1], 0.0)
-
-
-def close_fold(heat_next, salt_next, own, fold, area):
+    row = lax.broadcasted_iota(jnp.int32, (band, LANES), 0)
+    fields = ((heat_next, heat_out), (salt_next, salt_out))
+
+    def cells(rows, f):
+        return rows[f * levels : f * levels + levels]
+
+    @pl.when(pl.program_id(0) == 0)
+    def _():
+        for f, (before, after) in enumerate(fields):
+            flux = edge_flux(
+                cells(south_halo, f), cells(south_own, f), south_halo[base + 8 :],
+                south_halo[base : base + 1], south_own[base : base + 1], level,
+            )
+            entering = time_step / area[0:1] * flux
+            for k in range(levels):
+                after[k] = before[k] + jnp.where(row == 0, entering[k : k + 1], 0.0)
+
+    @pl.when(pl.program_id(0) == 1)
+    def _():
+        speed = 0.5 * (north_own[base + 8 :] - fold[base:])
+        wet = jnp.logical_and(level < north_own[base : base + 1], fold[levels:base] > 0.0)
+        forward, backward = jnp.maximum(speed, 0.0), jnp.minimum(speed, 0.0)
+        for f, (before, after) in enumerate(fields):
+            flux = jnp.where(wet, open_flux(cells(north_own, f), cells(fold, f), forward, backward), 0.0)
+            leaving = time_step / area[band - 1 : band] * flux
+            for k in range(levels):
+                after[k] = before[k] - jnp.where(row == band - 1, leaving[k : k + 1], 0.0)
+
+
+def close_edges(heat_next, salt_next, south_own, north_own, south_halo, fold, area):
     levels, height, width = heat_next.shape
-    band = pl.BlockSpec((levels, 8, width), lambda i: (0, height // 8 - 1, 0))
-    own_rows, fold_rows = (pl.BlockSpec(rows.shape, lambda i: (0, 0)) for rows in (own, fold))
-    return pl.pallas_call(
-        fold_kernel,
-        grid=(1,),
-        in_specs=[band, band, own_rows, fold_rows, pl.BlockSpec((8, width), lambda i: (height // 8 - 1, 0))],
+    gap = height // 8 - 1
+    band = pl.BlockSpec((levels, 8, width), lambda i: (0, i * gap, 0))
+    packs = (south_own, north_own, south_halo, fold)
+    return pl.pallas_call(
+        close_kernel,
+        grid=(2,),
+        in_specs=[band, band]
+        + [pl.BlockSpec(rows.shape, lambda i: (0, 0)) for rows in packs]
+        + [pl.BlockSpec((8, width), lambda i: (i * gap, 0))],
         out_specs=[band, band],
         out_shape=[jax.ShapeDtypeStruct(heat_next.shape, jnp.float32)] * 2,
         input_output_aliases={0: 0, 1: 1},
-        name="close_fold",
-    )(heat_next, salt_next, own, fold, area)
+        name="close_edges",
+    )(heat_next, salt_next, *packs, area)
 
 
 def final_kernel(salt_next, surface, rain, sea, totals, out):
@@ -290,8 +303,10 @@
             (i * height + height - 1, (3 * coarse - i) % around * height + height - 1) for i in range(around)
         ]
 
-        def branch(rows, arrays):
-            return lax.ppermute(rows, GX + ("gy",), pairs), beside(*arrays)
+        def branch(rows, arrays, south_own):
+            fold_halo = lax.ppermute(rows, GX + ("gy",), pairs)
+            north_halo = along(south_own, "gy", -1, False)
+            return fold_halo, beside(*arrays, north_halo)
 
         return branch
 
@@ -310,15 +325,16 @@
     totals = jnp.sum(totals, axis=0)
     west_halo = along(east_own, GX, 1, True)
     east_halo = along(west_own, GX, -1, True)
-    north_halo = along(south_own, "gy", -1, False)
     south_halo = along(north_own, "gy", 1, False)
     held = jnp.where(part == 0, west_halo[32:], jnp.where(part == 2, east_halo[24:], fold_own))
-    arrays = (
-        heat, brine, currents, sea, layers, area,
-        west_own, east_own, west_halo, east_halo, south_halo, north_halo,
-    )
-    fold_halo, (heat_next, salt_next) = lax.switch(place, fold_branches(tracer_step), held, arrays)
-    heat_next, salt_next = close_fold(heat_next, salt_next, north_own, fold_halo, area)
+    arrays = (heat, brine, currents, sea, layers, area, west_own, east_own, west_halo, east_halo)
+    fold_halo, (heat_next, salt_next) = lax.switch(
+        place, fold_branches(tracer_step), held, arrays, south_own
+    )
+    south_halo, fold_halo = lax.optimization_barrier((south_halo, fold_halo))
+    heat_next, salt_next = close_edges(
+        heat_next, salt_next, south_own, north_own, south_halo, fold_halo, area
+    )
     return heat_next, add_virtual(salt_next, brine, rain, sea, totals)
 
 

time: 94.6 us -> 97.5 us (1.031)
  the two profiles are of different devices: /device:TPU:38 before, /device:TPU:45 now
where the time goes in v4:
time: 97.5 us; the launch traced here: 96.9 us
  starting transfers between devices  59.7 us (61%)
  waiting for transfers between devices  21.1 us (22%)
  Pallas kernels  10.4 us (11%)
  local copies, waits for them, and re-layouts  3.99 us (4%)
  between operations  1.03 us (1%)
    all_to_all x2, starting transfers between devices, share(): return lax.all_to_all(copies, axes, 0, 0, tiled=True)  49.7 us
    ppermute x4, waiting for transfers between devices, along(): return lax.ppermute(block, axis, pairs)  21.1 us
    ppermute x4, starting transfers between devices, along(): return lax.ppermute(block, axis, pairs)  8.7 us
    pallas_call x1, Pallas kernels, tracer_step(): pl.pallas_call(step_kernel, in_specs=[VMEM] * 11, out_specs=[VMEM] * 2, o...  3.59 us
    pallas_call x1, Pallas kernels, packs(): pl.pallas_call(pack_kernel, in_specs=[VMEM] * 5, out_specs=[VMEM] * 5, ou...  3.55 us
    unnamed x24, local copies, waits for them, and re-layouts  2.78 us
  transfers between devices with their start and end apart: 7, of which 1 were waited for; matrix products, arithmetic and copies ran while one was open for 1% of the time, Pallas kernels for 6%

profile of v4, /device:TPU:45, one launch (start us, length us, event | category | flops | bytes accessed | tf_op | source)
XLA Modules:
  0.0 96.9 jit_solution(1501204567752781851)
XLA Ops:
  0.6 0.0 copy-start.33
  0.6 0.6 copy-done.33
  1.4 0.0 copy-start.5
  1.5 0.0 copy-start.3
  1.5 0.7 copy-done.5
  2.2 0.0 copy-done.3
  2.2 0.0 copy-start.1
  2.2 0.0 copy-start.4
  2.2 0.0 copy-start
  2.2 3.5 %edge_packs.1 = (f32[72,128]{1,0:T(8,128)S(1)}, f32[80,128]{1,0:T(8,128)S(1)}, f32[40,128]{1,0:T(8,128)S(1)}, f32[56,128]{1,0:T(8,128)}, f32[48,128]{1,0:T(8,128)}) custom-call(f32[16,64,128]{2,1,0:T(8,128)} %heat.1, f32[16,64,128]{2,1,0:T(8,128)} %surface.3, f32[2,16,64,128]{3,2,1,0:T(8,128)} %currents.1, s32[64,128]{1,0:T(8,128)S(1)} %copy-done.3, ...), custom_call_target="tpu_custom_call" | custom-call | tf_op jit(solution)/shard_map/edge_packs/pallas_call | solution.py:111
  5.8 0.0 copy-start.2
  5.8 3.0 %collective-permute-start.44 = (f32[80,128]{1,0:T(8,128)S(1)}, f32[80,128]{1,0:T(8,128)S(1)}, u32[]{:S(2)}, u32[]{:S(2)}) collective-permute-start(f32[80,128]{1,0:T(8,128)S(1)} %get-tuple-element.856), channel_id=1, source_target_pairs={{0,4},{4,8},{8,12},{12,16},{16,20},{20,24},{24,28},{28,32},{32,36}... | collective-permute-start | bytes 122888 | tf_op jit(solution)/shard_map/ppermute | solution.py:295
  8.8 0.0 copy-start.8
  8.8 0.0 collective-permute-start.45
  8.8 0.0 copy-done.1
  8.8 0.0 copy-done.4
  8.8 1.4 %local_sums.1 = f32[8,1,128]{2,1,0:T(1,128)} custom-call(f32[16,64,128]{2,1,0:T(8,128)S(1)} %copy-done.1, s32[64,128]{1,0:T(8,128)S(1)} %copy-done.3, f32[64,128]{1,0:T(8,128)S(1)} %copy-done.4, f32[64,128]{1,0:T(8,128)} %rain.3), custom_call_target="tpu_custom_call" | custom-call | tf_op jit(solution)/shard_map/local_sums/pallas_call | solution.py:41
  10.2 45.0 %all-to-all-start = ((f32[8,1,128]{2,1,0:T(1,128)}), f32[8,1,128]{2,1,0:T(1,128)S(1)}, u32[]{:S(2)}, u32[]{:S(2)}) async-start(f32[8,1,128]{2,1,0:T(1,128)} %local_sums.1), calls=%async_computation | async-start | bytes 8192 | tf_op jit(solution)/shard_map/all_to_all | solution.py:289
  55.2 0.0 copy-done.8
  55.2 2.8 %collective-permute-start.46 = (f32[56,128]{1,0:T(8,128)S(1)}, f32[56,128]{1,0:T(8,128)S(1)}, u32[]{:S(2)}, u32[]{:S(2)}) collective-permute-start(f32[56,128]{1,0:T(8,128)S(1)} %copy-done.8), channel_id=1, source_target_pairs={{0,1},{1,2},{2,3},{4,5},{5,6},{6,7},{8,9},{9,10},{10,11},{12,13},{... | collective-permute-start | bytes 86024 | tf_op jit(solution)/shard_map/ppermute | solution.py:295
  58.1 0.0 all-to-all-done
  58.1 0.0 copy-start.10
  58.1 0.6 broadcast_in_dim.2
  58.7 4.7 %all-to-all-start.1 = ((f32[32,1,128]{2,1,0:T(1,128)}), f32[32,1,128]{2,1,0:T(1,128)S(1)}, u32[]{:S(2)}, u32[]{:S(2)}) async-start(f32[32,1,128]{2,1,0:T(1,128)} %broadcast_in_dim.2), calls=%async_computation.1 | async-start | bytes 32768 | tf_op jit(solution)/shard_map/all_to_all | solution.py:289
  63.4 0.0 collective-permute-done.45
  63.5 0.0 collective-permute-done.44
  63.5 0.0 copy-done.10
  63.5 0.0 copy-done
  63.5 0.0 copy-done.2
  63.5 29.6 %conditional.1 = (f32[48,128]{1,0:T(8,128)}, f32[16,64,128]{2,1,0:T(8,128)S(1)}, f32[16,64,128]{2,1,0:T(8,128)S(1)}) conditional(s32[]{:T(128)} %clamp.3, (f32[48,128]{1,0:T(8,128)S(1)}, f32[40,128]{1,0:T(8,128)S(1)}, f32[16,64,128]{2,1,0:T(8,128)S(1)}, f32[16,64,128]{2,1,0:T(8,128)S(1)}, ...), branch_computations={%region_0.0_spmd, %region_1.2_spmd, %region_2.3_spmd, %region_3.4_... | conditional | bytes 262276 | solution.py:331
  63.5 1.3 %collective-permute-start.22 = (f32[48,128]{1,0:T(8,128)S(1)}, f32[48,128]{1,0:T(8,128)}, u32[]{:S(2)}, u32[]{:S(2)}) collective-permute-start(f32[48,128]{1,0:T(8,128)S(1)} %get-tuple-element.682), channel_id=1, source_target_pairs={{3,135},{7,131},{11,127},{15,123},{19,119},{23,115},{27,111},{31,1... | collective-permute-start | bytes 73736 | tf_op jit(solution)/shard_map/cond/branch_11_fun/ppermute | solution.py:307
  64.8 2.9 %collective-permute-start.23 = (f32[40,128]{1,0:T(8,128)S(1)}, f32[40,128]{1,0:T(8,128)S(1)}, u32[]{:S(2)}, u32[]{:S(2)}) collective-permute-start(f32[40,128]{1,0:T(8,128)S(1)} %get-tuple-element.693), channel_id=1, source_target_pairs={{1,0},{2,1},{3,2},{5,4},{6,5},{7,6},{9,8},{10,9},{11,10},{13,12},{... | collective-permute-start | bytes 61448 | tf_op jit(solution)/shard_map/cond/branch_11_fun/ppermute | solution.py:295
  67.7 21.1 %collective-permute-done.23.north_halo = f32[40,128]{1,0:T(8,128)S(1)} collective-permute-done((f32[40,128]{1,0:T(8,128)S(1)}, f32[40,128]{1,0:T(8,128)S(1)}, u32[]{:S(2)}, u32[]{:S(2)}) %collective-permute-start.23) | collective-permute-done | bytes 20512 | tf_op jit(solution)/shard_map/cond/branch_11_fun/ppermute | solution.py:295
  88.8 0.0 copy-start.22
  88.8 0.6 copy-done.22
  89.5 3.6 %tracer_step.33 = (f32[16,64,128]{2,1,0:T(8,128)S(1)}, f32[16,64,128]{2,1,0:T(8,128)S(1)}) custom-call(f32[16,64,128]{2,1,0:T(8,128)S(1)} %get-tuple-element.683.heat, f32[16,64,128]{2,1,0:T(8,128)S(1)} %get-tuple-element.684.salt, f32[2,16,64,128]{3,2,1,0:T(8,128)S(1)} %get-tuple-element.685.currents, s32[64,128]{1,0:T(8,128)S(1)} %get-tuple-element.686.sea, ...), custom_call_target="tpu_custom_call" | custom-call | tf_op jit(solution)/shard_map/cond/branch_11_fun/tracer_step/pallas_call | solution.py:198
  93.0 0.0 collective-permute-done.22
  93.1 0.0 collective-permute-done.46.south_halo
  93.1 0.0 copy-start.9
  93.1 0.6 copy-done.9
  93.7 0.9 close_edges.1
  94.6 0.0 copy-start.7
  94.7 0.0 all-to-all-done.1
  94.7 0.6 reduce_sum.21
  95.3 0.9 add_virtual.1
  96.1 0.0 copy-done.7
  96.1 0.0 copy-start.6
  96.1 0.8 copy-done.6
  (2 shorter events, 0.0 us)
Async XLA Ops:
  0.6 0.7 copy-start.33
  1.4 0.8 copy-start.5
  1.5 0.8 copy-start.3
  2.2 6.6 %copy-start.1 = (f32[16,64,128]{2,1,0:T(8,128)S(1)}, f32[16,64,128]{2,1,0:T(8,128)}, u32[]{:S(2)}) copy-start(f32[16,64,128]{2,1,0:T(8,128)} %surface.3) | copy-start | bytes 1572868
  2.2 6.6 %copy-start.4 = (f32[64,128]{1,0:T(8,128)S(1)}, f32[64,128]{1,0:T(8,128)}, u32[]{:S(2)}) copy-start(f32[64,128]{1,0:T(8,128)} %area.3) | copy-start | bytes 98308
  2.2 61.3 %copy-start = (f32[2,16,64,128]{3,2,1,0:T(8,128)S(1)}, f32[2,16,64,128]{3,2,1,0:T(8,128)}, u32[]{:S(2)}) copy-start(f32[2,16,64,128]{3,2,1,0:T(8,128)} %currents.1) | copy-start | bytes 3145732
  5.8 57.7 %copy-start.2 = (f32[16,64,128]{2,1,0:T(8,128)S(1)}, f32[16,64,128]{2,1,0:T(8,128)}, u32[]{:S(2)}) copy-start(f32[16,64,128]{2,1,0:T(8,128)} %heat.1) | copy-start | bytes 1572868
  5.8 57.7 %collective-permute-start.44 = (f32[80,128]{1,0:T(8,128)S(1)}, f32[80,128]{1,0:T(8,128)S(1)}, u32[]{:S(2)}, u32[]{:S(2)}) collective-permute-start(f32[80,128]{1,0:T(8,128)S(1)} %get-tuple-element.856), channel_id=1, source_target_pairs={{0,4},{4,8},{8,12},{12,16},{16,20},{20,24},{24,28},{28,32},{32,36}... | collective-permute-start | bytes 122888 | tf_op jit(solution)/shard_map/ppermute | solution.py:295
  8.8 46.5 %copy-start.8 = (f32[56,128]{1,0:T(8,128)S(1)}, f32[56,128]{1,0:T(8,128)}, u32[]{:S(2)}) copy-start(f32[56,128]{1,0:T(8,128)} %get-tuple-element.862.north_own) | copy-start | bytes 86020
  8.8 54.7 %collective-permute-start.45 = (f32[72,128]{1,0:T(8,128)S(1)}, f32[72,128]{1,0:T(8,128)S(1)}, u32[]{:S(2)}, u32[]{:S(2)}) collective-permute-start(f32[72,128]{1,0:T(8,128)S(1)} %get-tuple-element.857), channel_id=1, source_target_pairs={{0,252},{4,0},{8,4},{12,8},{16,12},{20,16},{24,20},{28,24},{32,28}... | collective-permute-start | bytes 110600 | tf_op jit(solution)/shard_map/ppermute | solution.py:295
  10.2 47.8 %all-to-all-start = ((f32[8,1,128]{2,1,0:T(1,128)}), f32[8,1,128]{2,1,0:T(1,128)S(1)}, u32[]{:S(2)}, u32[]{:S(2)}) async-start(f32[8,1,128]{2,1,0:T(1,128)} %local_sums.1), calls=%async_computation | async-start | bytes 8192 | tf_op jit(solution)/shard_map/all_to_all | solution.py:289
  55.2 37.9 %collective-permute-start.46 = (f32[56,128]{1,0:T(8,128)S(1)}, f32[56,128]{1,0:T(8,128)S(1)}, u32[]{:S(2)}, u32[]{:S(2)}) collective-permute-start(f32[56,128]{1,0:T(8,128)S(1)} %copy-done.8), channel_id=1, source_target_pairs={{0,1},{1,2},{2,3},{4,5},{5,6},{6,7},{8,9},{9,10},{10,11},{12,13},{... | collective-permute-start | bytes 86024 | tf_op jit(solution)/shard_map/ppermute | solution.py:295
  58.1 5.4 %copy-start.10 = (f32[48,128]{1,0:T(8,128)S(1)}, f32[48,128]{1,0:T(8,128)}, u32[]{:S(2)}) copy-start(f32[48,128]{1,0:T(8,128)} %get-tuple-element.858) | copy-start | bytes 73732
  58.7 35.9 %all-to-all-start.1 = ((f32[32,1,128]{2,1,0:T(1,128)}), f32[32,1,128]{2,1,0:T(1,128)S(1)}, u32[]{:S(2)}, u32[]{:S(2)}) async-start(f32[32,1,128]{2,1,0:T(1,128)} %broadcast_in_dim.2), calls=%async_computation.1 | async-start | bytes 32768 | tf_op jit(solution)/shard_map/all_to_all | solution.py:289
  63.5 29.5 %collective-permute-start.22 = (f32[48,128]{1,0:T(8,128)S(1)}, f32[48,128]{1,0:T(8,128)}, u32[]{:S(2)}, u32[]{:S(2)}) collective-permute-start(f32[48,128]{1,0:T(8,128)S(1)} %get-tuple-element.682), channel_id=1, source_target_pairs={{3,135},{7,131},{11,127},{15,123},{19,119},{23,115},{27,111},{31,1... | collective-permute-start | bytes 73736 | tf_op jit(solution)/shard_map/cond/branch_11_fun/ppermute | solution.py:307
  64.8 24.0 %collective-permute-start.23 = (f32[40,128]{1,0:T(8,128)S(1)}, f32[40,128]{1,0:T(8,128)S(1)}, u32[]{:S(2)}, u32[]{:S(2)}) collective-permute-start(f32[40,128]{1,0:T(8,128)S(1)} %get-tuple-element.693), channel_id=1, source_target_pairs={{1,0},{2,1},{3,2},{5,4},{6,5},{7,6},{9,8},{10,9},{11,10},{13,12},{... | collective-permute-start | bytes 61448 | tf_op jit(solution)/shard_map/cond/branch_11_fun/ppermute | solution.py:295
  88.8 0.6 copy-start.22
  93.1 0.6 copy-start.9
  94.6 1.5 %copy-start.7 = (f32[16,64,128]{2,1,0:T(8,128)}, f32[16,64,128]{2,1,0:T(8,128)S(1)}, u32[]{:S(2)}) copy-start(f32[16,64,128]{2,1,0:T(8,128)S(1)} %get-tuple-element.851) | copy-start | bytes 1572868
  96.1 0.8 copy-start.6
